TPU v7x, 128 devices: a whole 4x4x4 slice. The times are simulated.
128 devices in a mesh: dp: 1, sub: 2 (over core), ep: 64 (over z, y, x).
Axes of the slice: x: 4, y: 4, z: 4, core: 2. Of those that a mesh axis runs over, the one named last changes fastest.
Arguments:
- x: bfloat16 [65536, 1024], P(('dp', 'sub', 'ep'))
- route_idx: int32 [65536, 2], P(('dp', 'sub', 'ep'))
- route_gate: float32 [65536, 2], P(('dp', 'sub', 'ep'))
- w_gate: bfloat16 [128, 1024, 512], P(('sub', 'ep'))
- w_up: bfloat16 [128, 1024, 512], P(('sub', 'ep'))
- w_down: bfloat16 [128, 512, 1024], P(('sub', 'ep'))
Outputs:
- output: bfloat16 [65536, 1024], P(('dp', 'sub', 'ep'))
All inputs are finite; a program needn't handle non-finite values.
Results may differ from a plain program's by a relative error of at most 0.001.
Values are sent between devices in bfloat16 or wider.
A program may use at most 1 GiB of HBM per device.

v0:
```python
import jax
import jax.numpy as jnp
from jax import lax
from jax.sharding import PartitionSpec as P


def expert_ffn(tok_rows, w_gate, w_up, w_down):
    act_a = jnp.dot(tok_rows, w_gate, preferred_element_type=jnp.float32)
    act_b = jnp.dot(tok_rows, w_up, preferred_element_type=jnp.float32)
    hidden = (jax.nn.silu(act_a) * act_b).astype(jnp.bfloat16)
    return jnp.dot(hidden, w_down, preferred_element_type=jnp.float32).astype(jnp.bfloat16)


def pack_table(member, capacity):
    n_rows, n_dest = member.shape
    position = jnp.cumsum(member.astype(jnp.int32), axis=0) - 1
    target = jnp.where(member, jnp.arange(n_dest, dtype=jnp.int32)[None, :] * capacity + position, n_dest * capacity)
    source = jnp.broadcast_to(jnp.arange(n_rows, dtype=jnp.int32)[:, None], (n_rows, n_dest))
    slot_table = jnp.full((n_dest * capacity,), n_rows, jnp.int32).at[target.reshape(-1)].set(source.reshape(-1), mode='drop')
    return position, slot_table


def solution(mesh):
    n_sub = mesh.shape['sub']
    n_ep = mesh.shape['ep']
    n_dev = n_sub * n_ep
    tok_spec = P(('dp', 'sub', 'ep'), None)
    expert_spec = P(('sub', 'ep'), None, None)

    def device_step(x_loc, route_loc, gate_loc, w_gate, w_up, w_down):
        tok_dev, model_dim = x_loc.shape
        cap_pair = min(tok_dev, 8 * tok_dev // n_dev)
        cap_node = min(tok_dev, n_sub * cap_pair)
        cap_fwd = n_ep * cap_pair
        node_rows = n_ep * cap_node
        node_of = route_loc % n_ep
        to_node = jnp.any(node_of[:, :, None] == jnp.arange(n_ep, dtype=jnp.int32)[None, None, :], axis=1)
        pos_node, table_node = pack_table(to_node, cap_node)
        filled = table_node < tok_dev
        src_tok = jnp.minimum(table_node, tok_dev - 1)
        send_rows = jnp.where(filled[:, None], x_loc[src_tok], 0)
        picked = route_loc[src_tok]
        block_node = jnp.arange(node_rows, dtype=jnp.int32) // cap_node
        send_meta = jnp.where(filled[:, None] & (picked % n_ep == block_node[:, None]), picked // n_ep, -1)
        flat_rows = lax.all_to_all(send_rows.reshape(n_ep, cap_node, model_dim), 'ep', 0, 0).reshape(node_rows, model_dim)
        flat_meta = lax.all_to_all(send_meta.reshape(n_ep, cap_node, 2), 'ep', 0, 0).reshape(node_rows, 2)
        to_sub = jnp.any(flat_meta[:, :, None] == jnp.arange(n_sub, dtype=jnp.int32)[None, None, :], axis=1)
        pos_sub, table_sub = pack_table(to_sub, cap_fwd)
        fwd_ok = table_sub < node_rows
        fwd_rows = jnp.where(fwd_ok[:, None], flat_rows[jnp.minimum(table_sub, node_rows - 1)], 0)
        expert_in = lax.all_to_all(fwd_rows.reshape(n_sub, cap_fwd, model_dim), 'sub', 0, 0)
        expert_out = expert_ffn(expert_in.reshape(n_sub * cap_fwd, model_dim), w_gate[0], w_up[0], w_down[0])
        back_sub = lax.all_to_all(expert_out.reshape(n_sub, cap_fwd, model_dim), 'sub', 0, 0).reshape(n_sub * cap_fwd, model_dim)
        has_slot = flat_meta >= 0
        meta_safe = jnp.maximum(flat_meta, 0)
        slot_pos = jnp.maximum(jnp.take_along_axis(pos_sub, meta_safe, axis=1), 0)
        slot_rows = jnp.where(has_slot[:, :, None], back_sub[meta_safe * cap_fwd + slot_pos], 0)
        back_node = lax.all_to_all(slot_rows.reshape(n_ep, cap_node, 2, model_dim), 'ep', 0, 0).reshape(node_rows * 2, model_dim)
        my_pos = jnp.take_along_axis(pos_node, node_of, axis=1)
        got_rows = back_node[(node_of * cap_node + my_pos) * 2 + jnp.arange(2, dtype=jnp.int32)[None, :]].astype(jnp.float32)
        mixed = gate_loc[:, 0:1] * got_rows[:, 0] + gate_loc[:, 1:2] * got_rows[:, 1]
        return mixed.astype(jnp.bfloat16)

    return jax.shard_map(device_step, mesh=mesh, in_specs=(tok_spec, tok_spec, tok_spec, expert_spec, expert_spec, expert_spec), out_specs=tok_spec, check_vma=False)
```

profile of v0, /device:TPU:1, one launch (start us, length us, event | category | flops | bytes accessed | tf_op | source)
XLA Modules:
  0.0 833.7 jit_solution(12147466990908146037)
XLA Ops:
  5.4 120.0 %scatter_custom_fusion = s32[4096]{0:T(1024)S(1)} fusion(s32[32768]{0:T(1024)S(1)} %bitcast.101, s32[32768]{0:T(1024)S(1)} %reshape.306, s32[]{:T(128)} %constant.105.clone.1), kind=kCustom, calls=%fused_computation.75 | custom fusion | bytes 16388 | tf_op jit(solution)/shard_map/scatter | solution.py:19
  125.5 14.1 %gather_fusion = s32[4096,2]{1,0:T(8,128)} fusion(s32[512,2]{1,0:T(8,128)S(1)} %copy.69, s32[4096]{0:T(1024)S(1)} %fusion.13), kind=kCustom, calls=%fused_computation | custom fusion | bytes 81920 | tf_op jit(solution)/shard_map/gather | solution.py:42
  143.0 12.0 %all-to-all-start = ((s32[64,1,128]{2,1,0:T(1,128)}), s32[64,1,128]{2,1,0:T(1,128)S(1)}, u32[]{:S(2)}, u32[]{:S(2)}) async-start(s32[64,1,128]{2,1,0:T(1,128)} %reshape.347), calls=%async_computation | async-start | bytes 65536 | tf_op jit(solution)/shard_map/all_to_all | solution.py:46
  155.0 18.3 %gather_fusion.1 = bf16[4096,1024]{1,0:T(8,128)(2,1)} fusion(bf16[512,1024]{1,0:T(8,128)(2,1)S(1)} %copy-done, s32[4096]{0:T(1024)S(1)} %fusion.13), kind=kCustom, calls=%fused_computation.1 | custom fusion | bytes 16793600 | tf_op jit(solution)/shard_map/gather | solution.py:41
  173.3 7.2 broadcast_select_fusion.1
  180.5 10.2 %all-to-all-start.1 = ((bf16[64,64,1024]{2,1,0:T(8,128)(2,1)}), bf16[64,64,1024]{2,1,0:T(8,128)(2,1)}, u32[]{:S(2)}, u32[]{:S(2)}) async-start(bf16[64,64,1024]{2,1,0:T(8,128)(2,1)} %broadcast_select_fusion.1), calls=%async_computation.1 | async-start | bytes 16777216 | tf_op jit(solution)/shard_map/all_to_all | solution.py:45
  205.3 69.0 %gather_fusion.5 = s32[8192]{0:T(1024)S(1)} fusion(s32[4096,2]{0,1:T(2,128)S(1)} %bitcast.91, s32[8192]{0:T(1024)S(1)} %reshape.290), kind=kCustom, calls=%fused_computation.5 | custom fusion | bytes 131072 | tf_op jit(solution)/shard_map/jit(take_along_axis)/gather | solution.py:56
  289.9 30.9 %scatter_custom_fusion.1 = s32[4096]{0:T(1024)S(1)} fusion(s32[8192]{0:T(1024)S(1)} %bitcast.103, s32[8192]{0:T(1024)} %reshape.314, s32[]{:T(128)} %constant.111.clone.1), kind=kCustom, calls=%fused_computation.72 | custom fusion | bytes 16896 | tf_op jit(solution)/shard_map/scatter | solution.py:19
  320.8 25.4 %gather_fusion.2 = bf16[4096,1024]{1,0:T(8,128)(2,1)} fusion(bf16[4096,1024]{1,0:T(8,128)(2,1)} %bitcast.10, s32[4096]{0:T(1024)S(1)} %fusion.14), kind=kCustom, calls=%fused_computation.2 | custom fusion | bytes 16793600 | tf_op jit(solution)/shard_map/gather | solution.py:50
  346.2 4.4 broadcast_select_fusion.2
  350.7 11.8 %all_to_all.25 = bf16[2,2048,1024]{2,1,0:T(8,128)(2,1)S(1)} all-to-all(bf16[2,2048,1024]{2,1,0:T(8,128)(2,1)S(1)} %broadcast_select_fusion.2), channel_id=1, replica_groups=mesh['dp'=1,'sub'=2,'ep'=64] {'sub'}, dimensions={0} | all-to-all | bytes 16777216 | tf_op jit(solution)/shard_map/all_to_all | solution.py:51
  365.7 6.7 fusion.8
  372.4 15.5 %convolution_convert_fusion = bf16[4096,1024]{1,0:T(8,128)(2,1)} fusion(f32[4096,512]{1,0:T(8,128)} %fusion.8, bf16[4096,1024]{1,0:T(8,128)(2,1)} %bitcast.97, bf16[1,512,1024]{2,1,0:T(8,128)(2,1)S(1)} %copy-done.18, bf16[1,1024,512]{2,1,0:T(8,128)(2,1)S(1)} %copy-done.19), kind=kOutput, calls=%fused_computation.13 | convolution fusion | flops 8606711808 | bytes 27262976 | tf_op jit(solution)/shard_map/dot_general | solution.py:11
  387.9 18.2 %all_to_all.26 = bf16[2,2048,1024]{2,1,0:T(8,128)(2,1)} all-to-all(bf16[2,2048,1024]{2,1,0:T(8,128)(2,1)} %bitcast.98), channel_id=1, replica_groups=mesh['dp'=1,'sub'=2,'ep'=64] {'sub'}, dimensions={0} | all-to-all | bytes 16777216 | tf_op jit(solution)/shard_map/all_to_all | solution.py:53
  406.1 45.3 %gather_fusion.3 = bf16[8192,1024]{1,0:T(8,128)(2,1)} fusion(bf16[4096,1024]{1,0:T(8,128)(2,1)} %bitcast.93, s32[8192]{0:T(1024)S(1)} %broadcast_clamp_fusion), kind=kCustom, calls=%fused_computation.3 | custom fusion | bytes 33587200 | tf_op jit(solution)/shard_map/gather | solution.py:57
  451.4 25.0 %gather.42 = bf16[64,64,2,1024]{3,2,1,0:T(2,128)(2,1)} reshape(bf16[8192,1024]{1,0:T(8,128)(2,1)} %gather_fusion.3) | data formatting | bytes 33554432 | tf_op jit(solution)/shard_map/gather | solution.py:57
  476.4 20.3 %broadcast_select_fusion = bf16[64,64,2,1024]{3,2,1,0:T(2,128)(2,1)} fusion(bf16[64,64,2,1024]{3,2,1,0:T(2,128)(2,1)} %gather.42, pred[64,64,2]{2,1,0:T(8,128)(4,1)S(1)} %copy-done.7), kind=kLoop, calls=%fused_computation.9 | loop fusion | flops 8388608 | bytes 33562624 | tf_op jit(solution)/shard_map/jit(_where)/select_n | solution.py:57
  496.6 10.6 %all-to-all-start.4 = ((bf16[64,64,2,1024]{3,2,1,0:T(2,128)(2,1)}), bf16[64,64,2,1024]{3,2,1,0:T(2,128)(2,1)}, u32[]{:S(2)}, u32[]{:S(2)}) async-start(bf16[64,64,2,1024]{3,2,1,0:T(2,128)(2,1)} %broadcast_select_fusion), calls=%async_computation.4 | async-start | bytes 33554432 | tf_op jit(solution)/shard_map/all_to_all | solution.py:58
  508.2 7.1 gather_fusion.6
  515.8 266.8 %all-to-all-done.4 = bf16[64,64,2,1024]{3,2,1,0:T(2,128)(2,1)} async-done(((bf16[64,64,2,1024]{3,2,1,0:T(2,128)(2,1)}), bf16[64,64,2,1024]{3,2,1,0:T(2,128)(2,1)}, u32[]{:S(2)}, u32[]{:S(2)}) %all-to-all-start.4) | async-done | bytes 16777248 | tf_op jit(solution)/shard_map/all_to_all | solution.py:58
  782.6 24.9 %reshape.246 = bf16[8192,1024]{1,0:T(8,128)(2,1)} reshape(bf16[64,64,2,1024]{3,2,1,0:T(2,128)(2,1)} %all-to-all-done.4) | data formatting | bytes 33554432 | tf_op jit(solution)/shard_map/reshape | solution.py:58
  807.5 12.9 %gather_fusion.4 = bf16[1024,1024]{1,0:T(8,128)(2,1)S(1)} fusion(bf16[8192,1024]{1,0:T(8,128)(2,1)} %reshape.246, s32[1024]{0:T(1024)S(1)} %broadcast_clamp_fusion.1), kind=kCustom, calls=%fused_computation.4 | custom fusion | bytes 4198400 | tf_op jit(solution)/shard_map/gather | solution.py:60
  820.5 4.0 reshape.330
  824.5 7.1 fusion.20
  (111 shorter events, 45.0 us)
Async XLA Ops:
  0.0 154.9 %copy-start = (bf16[512,1024]{1,0:T(8,128)(2,1)S(1)}, bf16[512,1024]{1,0:T(8,128)(2,1)}, u32[]{:S(2)}) copy-start(bf16[512,1024]{1,0:T(8,128)(2,1)} %param.6) | copy-start | bytes 3145732
  2.8 2.0 copy-start.5
  5.0 134.7 %copy-start.2 = (s32[64,4,128]{0,2,1:T(8,128)}, s32[64,4,128]{0,2,1:T(8,128)S(1)}, u32[]{:S(2)}) copy-start(s32[64,4,128]{0,2,1:T(8,128)S(1)} %copy.91) | copy-start | bytes 393220
  143.0 37.5 %all-to-all-start = ((s32[64,1,128]{2,1,0:T(1,128)}), s32[64,1,128]{2,1,0:T(1,128)S(1)}, u32[]{:S(2)}, u32[]{:S(2)}) async-start(s32[64,1,128]{2,1,0:T(1,128)} %reshape.347), calls=%async_computation | async-start | bytes 65536 | tf_op jit(solution)/shard_map/all_to_all | solution.py:46
  180.5 140.3 %all-to-all-start.1 = ((bf16[64,64,1024]{2,1,0:T(8,128)(2,1)}), bf16[64,64,1024]{2,1,0:T(8,128)(2,1)}, u32[]{:S(2)}, u32[]{:S(2)}) async-start(bf16[64,64,1024]{2,1,0:T(8,128)(2,1)} %broadcast_select_fusion.1), calls=%async_computation.1 | async-start | bytes 16777216 | tf_op jit(solution)/shard_map/all_to_all | solution.py:45
  194.8 0.6 copy-start.13
  196.4 8.8 %copy-start.10 = (s32[1,2,32,128]{3,2,1,0:T(8,128)}, s32[1,2,32,128]{3,2,1,0:T(8,128)S(1)}, u32[]{:S(2)}) copy-start(s32[1,2,32,128]{3,2,1,0:T(8,128)S(1)} %add_bitcast_fusion) | copy-start | bytes 98308
  205.2 71.1 %copy-start.11 = (s32[1,2,32,128]{3,2,1,0:T(8,128)S(1)}, s32[1,2,32,128]{3,2,1,0:T(8,128)}, u32[]{:S(2)}) copy-start(s32[1,2,32,128]{3,2,1,0:T(8,128)} %copy-done.10) | copy-start | bytes 98308
  205.2 71.1 %copy-start.14 = (pred[4096,2]{0,1:T(4,128)(4,1)S(1)}, pred[4096,2]{0,1:T(4,128)(4,1)}, u32[]{:S(2)}) copy-start(pred[4096,2]{0,1:T(4,128)(4,1)} %copy-done.13) | copy-start | bytes 24580
  205.3 71.1 %copy-start.16 = (s32[2]{0:T(128)S(1)}, s32[2]{0:T(128)}, u32[]{:S(2)}) copy-start(s32[2]{0:T(128)} %iota_multiply_fusion) | copy-start | bytes 28
  274.3 7.3 copy-start.12
  274.3 9.3 %copy-start.8 = (pred[64,64,2]{2,1,0:T(8,128)(4,1)S(1)}, pred[64,64,2]{2,1,0:T(8,128)(4,1)}, u32[]{:S(2)}) copy-start(pred[64,64,2]{2,1,0:T(8,128)(4,1)} %copy.87) | copy-start | bytes 24580
  350.7 15.0 %copy-start.17 = (bf16[1,1024,512]{2,1,0:T(8,128)(2,1)S(1)}, bf16[1,1024,512]{2,1,0:T(8,128)(2,1)}, u32[]{:S(2)}) copy-start(bf16[1,1024,512]{2,1,0:T(8,128)(2,1)} %param.9) | copy-start | bytes 3145732
  362.5 3.2 copy-start.4
  365.7 6.7 copy-start.18
  365.7 6.7 copy-start.19
  451.4 25.0 %copy-start.7 = (pred[64,64,2]{2,1,0:T(8,128)(4,1)S(1)}, pred[64,64,2]{2,1,0:T(8,128)(4,1)}, u32[]{:S(2)}) copy-start(pred[64,64,2]{2,1,0:T(8,128)(4,1)} %copy.83) | copy-start | bytes 24580
  496.6 10.6 %copy-start.9 = (s32[512,2,1]{1,0,2:T(8,128)S(1)}, s32[512,2,1]{1,0,2:T(8,128)}, u32[]{:S(2)}) copy-start(s32[512,2,1]{1,0,2:T(8,128)} %get-tuple-element.5) | copy-start | bytes 12292
  496.6 286.0 %all-to-all-start.4 = ((bf16[64,64,2,1024]{3,2,1,0:T(2,128)(2,1)}), bf16[64,64,2,1024]{3,2,1,0:T(2,128)(2,1)}, u32[]{:S(2)}, u32[]{:S(2)}) async-start(bf16[64,64,2,1024]{3,2,1,0:T(2,128)(2,1)} %broadcast_select_fusion), calls=%async_computation.4 | async-start | bytes 33554432 | tf_op jit(solution)/shard_map/all_to_all | solution.py:58
  507.2 1.0 copy-start.3
  508.2 7.3 copy-start.6
  508.2 7.6 copy-start.15
  824.4 8.8 %copy-start.1 = (bf16[512,1024]{1,0:T(8,128)(2,1)S(1)}, bf16[512,1024]{1,0:T(8,128)(2,1)}, u32[]{:S(2)}) copy-start(bf16[512,1024]{1,0:T(8,128)(2,1)} %param.6) | copy-start | bytes 3145732
where the time goes:
time: 850 us; the launch traced here: 834 us
  local copies, waits for them, and re-layouts  435 us (51%)
  waiting for transfers between devices  267 us (31%)
  other arithmetic  45.4 us (5%)
  starting transfers between devices  32.8 us (4%)
  blocking collectives  30 us (4%)
  matrix products  22.2 us (3%)
    all_to_all x1, waiting for transfers between devices, device_step(): lax.all_to_all(slot_rows.reshape(n_ep, cap_node, 2, model_dim), 'ep', 0, 0)  267 us
    scatter x2, local copies, waits for them, and re-layouts, pack_table(): jnp.full((n_dest * capacity,), n_rows, jnp.int32).at[target.reshape(-1)]  151 us
    gather x4, local copies, waits for them, and re-layouts, device_step(): slot_pos = jnp.maximum(jnp.take_along_axis(pos_sub, meta_safe, axis=1), 0)  74.5 us
    gather x2, local copies, waits for them, and re-layouts, device_step(): back_sub[meta_safe * cap_fwd + slot_pos]  70.2 us
    gather x1, local copies, waits for them, and re-layouts, device_step(): flat_rows[jnp.minimum(table_sub, node_rows - 1)]  25.4 us
    reshape x1, local copies, waits for them, and re-layouts, device_step(): lax.all_to_all(slot_rows.reshape(n_ep, cap_node, 2, model_dim), 'ep', 0, 0)  24.9 us
    select_n x1, other arithmetic, device_step(): jnp.where(has_slot[:, :, None], back_sub[meta_safe * cap_fwd + slot_pos], 0)  20.3 us
    gather x1, local copies, waits for them, and re-layouts, device_step(): send_rows = jnp.where(filled[:, None], x_loc[src_tok], 0)  18.3 us
  transfers between devices with their start and end apart: 3, of which 1 were waited for; matrix products, arithmetic and copies ran while one was open for 19% of the time, Pallas kernels for 0%

commit v1 on v0

v1 whole, which is shorter than its diff:
```python
import functools

import jax
import jax.numpy as jnp
from jax import lax
from jax.experimental import pallas as pl
from jax.experimental.pallas import tpu as pltpu
from jax.sharding import PartitionSpec as P

TILE = 256
VMEM_LIMIT = 56 * 1024 * 1024


def iota(shape, dim):
    return lax.broadcasted_iota(jnp.int32, shape, dim)


def ones_where(mask):
    return jnp.where(mask, 1.0, 0.0).astype(jnp.bfloat16)


def dot(a, b):
    return jnp.dot(a, b, preferred_element_type=jnp.float32)


def pack_kernel(cap, route_ref, x_ref, send_ref, pos_ref):
    tok = x_ref.shape[0]
    rows = send_ref.shape[0]
    lanes = iota((tok, rows // cap), 1)
    member0 = ones_where(route_ref[:, 0:1] == lanes)
    member1 = ones_where(route_ref[:, 1:2] == lanes)
    lower = ones_where(iota((tok, tok), 0) >= iota((tok, tok), 1))
    rank0 = dot(lower, member0)
    rank1 = dot(lower, member1) + rank0[tok - 1:tok, :]
    base = (lanes * cap - 1).astype(jnp.float32)
    pos0 = jnp.sum(jnp.where(member0 > 0, rank0 + base, 0.0), axis=1, keepdims=True)
    pos1 = jnp.sum(jnp.where(member1 > 0, rank1 + base, 0.0), axis=1, keepdims=True)
    pos_ref[...] = jnp.concatenate([pos0, pos1], axis=1).astype(jnp.int32)
    row0 = jnp.transpose(jnp.broadcast_to(pos0, (tok, 128)))[0:1, :]
    row1 = jnp.transpose(jnp.broadcast_to(pos1, (tok, 128)))[0:1, :]

    def block(i, carry):
        place = (iota((TILE, tok), 0) + i * TILE).astype(jnp.float32)
        pick = ones_where((place == row0) | (place == row1))
        send_ref[pl.ds(pl.multiple_of(i * TILE, TILE), TILE), :] = dot(pick, x_ref[...]).astype(jnp.bfloat16)
        return carry

    lax.fori_loop(0, rows // TILE, block, 0)


def ffn_kernel(x_ref, wg_ref, wu_ref, wd_ref, o_ref):
    rows = x_ref[...]
    act_a = dot(rows, wg_ref[...])
    act_b = dot(rows, wu_ref[...])
    hidden = (jax.nn.silu(act_a) * act_b).astype(jnp.bfloat16)
    o_ref[...] = dot(hidden, wd_ref[...]).astype(jnp.bfloat16)


def mix_kernel(ret_ref, pos_ref, gate_ref, y_ref):
    n_rows = ret_ref.shape[0]
    tok = y_ref.shape[0]
    for block in range(tok // TILE):
        part = pl.ds(block * TILE, TILE)
        lanes = iota((TILE, n_rows), 1)
        total = gate_ref[part, 0:1] * dot(ones_where(pos_ref[part, 0:1] == lanes), ret_ref[...])
        total = total + gate_ref[part, 1:2] * dot(ones_where(pos_ref[part, 1:2] == lanes), ret_ref[...])
        y_ref[part, :] = total.astype(jnp.bfloat16)


def solution(mesh):
    n_dev = mesh.shape["sub"] * mesh.shape["ep"]
    tok_spec = P(("dp", "sub", "ep"), None)
    expert_spec = P(("sub", "ep"), None, None)
    group = ("sub", "ep")
    vmem = pl.BlockSpec(memory_space=pltpu.VMEM)
    params = pltpu.CompilerParams(vmem_limit_bytes=VMEM_LIMIT)

    def device_step(x, route, gate, w_gate, w_up, w_down):
        tok, dim = x.shape
        ff = w_gate.shape[2]
        cap = min(tok, 8 * tok // n_dev)
        rows = n_dev * cap
        buffer = jax.ShapeDtypeStruct((rows, dim), jnp.bfloat16)
        send, pos = pl.pallas_call(
            functools.partial(pack_kernel, cap),
            out_shape=[buffer, jax.ShapeDtypeStruct((tok, 2), jnp.int32)],
            in_specs=[vmem, vmem],
            out_specs=[vmem, vmem],
            compiler_params=params,
            name="pack",
        )(route, x)
        got = lax.all_to_all(send.reshape(n_dev, cap, dim), group, 0, 0).reshape(rows, dim)
        out = pl.pallas_call(
            ffn_kernel,
            out_shape=buffer,
            grid=(rows // TILE,),
            in_specs=[
                pl.BlockSpec((TILE, dim), lambda i: (i, 0)),
                pl.BlockSpec((dim, ff), lambda i: (0, 0)),
                pl.BlockSpec((dim, ff), lambda i: (0, 0)),
                pl.BlockSpec((ff, dim), lambda i: (0, 0)),
            ],
            out_specs=pl.BlockSpec((TILE, dim), lambda i: (i, 0)),
            compiler_params=params,
            name="ffn",
        )(got, w_gate[0], w_up[0], w_down[0])
        ret = lax.all_to_all(out.reshape(n_dev, cap, dim), group, 0, 0).reshape(rows, dim)
        return pl.pallas_call(
            mix_kernel,
            out_shape=jax.ShapeDtypeStruct((tok, dim), jnp.bfloat16),
            in_specs=[vmem, vmem, vmem],
            out_specs=vmem,
            compiler_params=params,
            name="mix",
        )(ret, pos, gate)

    return jax.shard_map(
        device_step,
        mesh=mesh,
        in_specs=(tok_spec, tok_spec, tok_spec, expert_spec, expert_spec, expert_spec),
        out_specs=tok_spec,
        check_vma=False,
    )
```

time: 850 us -> 327 us (0.38); the launches traced: 834 us -> 323 us
  local copies, waits for them, and re-layouts: 435 us -> 2.39 us
  waiting for transfers between devices: 267 us -> 132 us
  blocking collectives: 30 us -> 130 us
  Pallas kernels: 0 us -> 47.2 us
  other arithmetic: 45.4 us -> 0 us
  matrix products: 22.2 us -> 0 us
  starting transfers between devices: 32.8 us -> 11.1 us
    gather x14 -> x0, local copies, waits for them, and re-layouts: 225 us -> none  [the longest x4 74.5 us: device_step(): slot_pos = jnp.maximum(jnp.take_along_axis(pos_sub, meta_safe, axis=1), 0)]
    scatter x2 -> x0, local copies, waits for them, and re-layouts: 151 us -> none  [pack_table(): jnp.full((n_dest * capacity,), n_rows, jnp.int32).at[target.reshape(-1)]]
    all_to_all x3 -> x1, waiting for transfers between devices: 267 us -> 132 us  [device_step(): lax.all_to_all(out.reshape(n_dev, cap, dim), group, 0, 0).reshape(rows, dim)]
    all_to_all x2 -> x1, blocking collectives: 30 us -> 130 us  [device_step(): lax.all_to_all(send.reshape(n_dev, cap, dim), group, 0, 0)]
    pallas_call x0 -> x3, Pallas kernels: none -> 47.2 us  [the longest x1 21.3 us: device_step(): pl.pallas_call(ffn_kernel, out_shape=buffer, grid=(rows // TILE,), in_spe...]
    select_n x10 -> x0, other arithmetic: 35.8 us -> none  [the longest x1 20.3 us: device_step(): jnp.where(has_slot[:, :, None], back_sub[meta_safe * cap_fwd + slot_pos], 0)]
    reshape x5 -> x0, local copies, waits for them, and re-layouts: 30.1 us -> none  [the longest x1 24.9 us: device_step(): lax.all_to_all(slot_rows.reshape(n_ep, cap_node, 2, model_dim), 'ep', 0, 0)]
    dot_general x2 -> x0, matrix products: 22.2 us -> none  [the longest x1 15.5 us: expert_ffn(): jnp.dot(hidden, w_down, preferred_element_type=jnp.float32)]
  transfers between devices with their start and end apart: 3 -> 1, of which waited for: 1 -> 1; matrix products, arithmetic and copies ran while one was open for 19% -> 0% of each run, Pallas kernels for 0% -> 0%
where the time goes in v1:
time: 327 us; the launch traced here: 323 us
  waiting for transfers between devices  132 us (40%)
  blocking collectives  130 us (40%)
  Pallas kernels  47.2 us (14%)
  starting transfers between devices  11.1 us (3%)
    all_to_all x1, waiting for transfers between devices, device_step(): lax.all_to_all(out.reshape(n_dev, cap, dim), group, 0, 0).reshape(rows, dim)  132 us
    all_to_all x1, blocking collectives, device_step(): lax.all_to_all(send.reshape(n_dev, cap, dim), group, 0, 0)  130 us
    pallas_call x1, Pallas kernels, device_step(): pl.pallas_call(ffn_kernel, out_shape=buffer, grid=(rows // TILE,), in_spe...  21.3 us
    pallas_call x1, Pallas kernels, device_step(): pl.pallas_call(mix_kernel, out_shape=jax.ShapeDtypeStruct((tok, dim), jnp...  13.4 us
    pallas_call x1, Pallas kernels, device_step(): pl.pallas_call(functools.partial(pack_kernel, cap), out_shape=[buffer, ja...  12.6 us
    all_to_all x1, starting transfers between devices, device_step(): lax.all_to_all(out.reshape(n_dev, cap, dim), group, 0, 0).reshape(rows, dim)  11.1 us
  transfers between devices with their start and end apart: 1, of which 1 were waited for; matrix products, arithmetic and copies ran while one was open for 0% of the time, Pallas kernels for 0%

profile of v1, /device:TPU:1, one launch (start us, length us, event | category | flops | bytes accessed | tf_op | source)
XLA Modules:
  0.0 323.4 jit_solution(17445879472949423731)
XLA Ops:
  0.0 1.5 copy.7.route_ref
  1.5 12.6 %pack.1 = (bf16[4096,1024]{1,0:T(8,128)(2,1)}, s32[512,2]{1,0:T(8,128)}) custom-call(s32[512,2]{1,0:T(8,128)} %copy.7.route_ref, bf16[512,1024]{1,0:T(8,128)(2,1)} %x_ref.1), custom_call_target="tpu_custom_call" | custom-call | tf_op jit(solution)/shard_map/pack/pallas_call | solution.py:84
  14.1 130.5 %all_to_all.10 = bf16[128,32,1024]{2,1,0:T(8,128)(2,1)} all-to-all(bf16[128,32,1024]{2,1,0:T(8,128)(2,1)} %bitcast.9), channel_id=1, replica_groups=mesh['dp'=1,'sub'=2,'ep'=64] {'sub','ep'}, dimensions={0} | all-to-all | bytes 16777216 | tf_op jit(solution)/shard_map/all_to_all | solution.py:92
  144.6 21.3 %ffn.1 = bf16[4096,1024]{1,0:T(8,128)(2,1)} custom-call(bf16[4096,1024]{1,0:T(8,128)(2,1)} %bitcast.8, bf16[1024,512]{1,0:T(8,128)(2,1)} %bitcast.10, bf16[1024,512]{1,0:T(8,128)(2,1)} %bitcast.11, bf16[512,1024]{1,0:T(8,128)(2,1)} %bitcast.12), custom_call_target="tpu_custom_call" | custom-call | tf_op jit(solution)/shard_map/ffn/pallas_call | solution.py:93
  165.9 0.0 copy-start
  165.9 11.1 %all-to-all-start.1 = ((bf16[128,32,1024]{2,1,0:T(8,128)(2,1)}), bf16[128,32,1024]{2,1,0:T(8,128)(2,1)}, u32[]{:S(2)}, u32[]{:S(2)}) async-start(bf16[128,32,1024]{2,1,0:T(8,128)(2,1)} %bitcast.7), calls=%async_computation.1 | async-start | bytes 16777216 | tf_op jit(solution)/shard_map/all_to_all | solution.py:107
  177.0 0.0 copy-done
  177.0 0.9 copy.8.gate_ref
  177.8 132.2 %all-to-all-done.1 = bf16[128,32,1024]{2,1,0:T(8,128)(2,1)} async-done(((bf16[128,32,1024]{2,1,0:T(8,128)(2,1)}), bf16[128,32,1024]{2,1,0:T(8,128)(2,1)}, u32[]{:S(2)}, u32[]{:S(2)}) %all-to-all-start.1) | async-done | bytes 8388640 | tf_op jit(solution)/shard_map/all_to_all | solution.py:107
  310.1 13.4 %mix.1 = bf16[512,1024]{1,0:T(8,128)(2,1)} custom-call(bf16[4096,1024]{1,0:T(8,128)(2,1)} %bitcast.6.ret_ref, s32[512,2]{1,0:T(8,128)} %get-tuple-element.8.pos_ref, f32[512,2]{1,0:T(8,128)} %copy.8.gate_ref), custom_call_target="tpu_custom_call" | custom-call | tf_op jit(solution)/shard_map/mix/pallas_call | solution.py:108
Async XLA Ops:
  165.9 11.1 %copy-start = (f32[512,2]{0,1:T(2,128)S(1)}, f32[512,2]{0,1:T(2,128)}, u32[]{:S(2)}) copy-start(f32[512,2]{0,1:T(2,128)} %param.8) | copy-start | bytes 12292
  165.9 144.1 %all-to-all-start.1 = ((bf16[128,32,1024]{2,1,0:T(8,128)(2,1)}), bf16[128,32,1024]{2,1,0:T(8,128)(2,1)}, u32[]{:S(2)}, u32[]{:S(2)}) async-start(bf16[128,32,1024]{2,1,0:T(8,128)(2,1)} %bitcast.7), calls=%async_computation.1 | async-start | bytes 16777216 | tf_op jit(solution)/shard_map/all_to_all | solution.py:107

commit v2 on v1

v2 whole, which is shorter than its diff:
```python
import functools

import jax
import jax.numpy as jnp
from jax import lax
from jax.experimental import pallas as pl
from jax.experimental.pallas import tpu as pltpu
from jax.sharding import PartitionSpec as P

MESH = pl.DeviceIdType.MESH
TILE = 256
VMEM_LIMIT = 60 * 1024 * 1024
COLORS = 3
PART = 4
BASE = COLORS * PART
SPARE = 8
OVER = COLORS * SPARE
SIDE = 4
TAIL = 128


def iota(shape, dim):
    return lax.broadcasted_iota(jnp.int32, shape, dim)


def ones_where(mask):
    return jnp.where(mask, 1.0, 0.0).astype(jnp.bfloat16)


def dot(a, b):
    return jnp.dot(a, b, preferred_element_type=jnp.float32)


def expert_ffn(rows, wg_ref, wu_ref, wd_ref):
    act_a = dot(rows, wg_ref[...])
    act_b = dot(rows, wu_ref[...])
    hidden = (jax.nn.silu(act_a) * act_b).astype(jnp.bfloat16)
    return dot(hidden, wd_ref[...]).astype(jnp.bfloat16)


def ranks(route_ref, n_experts):
    tok = route_ref.shape[0]
    lanes = iota((tok, n_experts), 1)
    member0 = route_ref[:, 0:1] == lanes
    member1 = route_ref[:, 1:2] == lanes
    lower = ones_where(iota((tok, tok), 0) >= iota((tok, tok), 1))
    rank0 = dot(lower, ones_where(member0))
    rank1 = dot(lower, ones_where(member1)) + rank0[tok - 1:tok, :]
    return member0, member1, rank0 - 1.0, rank1 - 1.0, rank1[tok - 1:tok, :]


def as_row(column):
    return jnp.transpose(jnp.broadcast_to(column, (column.shape[0], 128)))[0:1, :]


def wide_pack_kernel(cap, route_ref, x_ref, send_ref, pos_ref):
    tok = x_ref.shape[0]
    rows = send_ref.shape[0]
    member0, member1, rank0, rank1, _ = ranks(route_ref, rows // cap)
    base = (iota(member0.shape, 1) * cap).astype(jnp.float32)
    pos0 = jnp.sum(jnp.where(member0, rank0 + base, 0.0), axis=1, keepdims=True)
    pos1 = jnp.sum(jnp.where(member1, rank1 + base, 0.0), axis=1, keepdims=True)
    pos_ref[...] = jnp.concatenate([pos0, pos1], axis=1).astype(jnp.int32)
    row0, row1 = as_row(pos0), as_row(pos1)

    def block(i, carry):
        place = (iota((TILE, tok), 0) + i * TILE).astype(jnp.float32)
        pick = ones_where((place == row0) | (place == row1))
        send_ref[pl.ds(pl.multiple_of(i * TILE, TILE), TILE), :] = dot(pick, x_ref[...]).astype(jnp.bfloat16)
        return carry

    lax.fori_loop(0, rows // TILE, block, 0)


def wide_ffn_kernel(x_ref, wg_ref, wu_ref, wd_ref, o_ref):
    o_ref[...] = expert_ffn(x_ref[...], wg_ref, wu_ref, wd_ref)


def wide_mix_kernel(ret_ref, pos_ref, gate_ref, y_ref):
    n_rows = ret_ref.shape[0]

    def block(i, carry):
        part = pl.ds(pl.multiple_of(i * TILE, TILE), TILE)
        lanes = iota((TILE, n_rows), 1)
        total = gate_ref[part, 0:1] * dot(ones_where(pos_ref[part, 0:1] == lanes), ret_ref[...])
        total = total + gate_ref[part, 1:2] * dot(ones_where(pos_ref[part, 1:2] == lanes), ret_ref[...])
        y_ref[part, :] = total.astype(jnp.bfloat16)
        return carry

    lax.fori_loop(0, y_ref.shape[0] // TILE, block, 0)


def pack_kernel(route_ref, x_ref, send_ref, over_ref, pos_ref):
    tok, dim = x_ref.shape
    n_experts = send_ref.shape[1]
    rows = n_experts * PART
    member0, member1, rank0, rank1, count = ranks(route_ref, n_experts)
    lanes = iota((1, n_experts), 1)
    sub, ep = lanes // (SIDE ** 3), lanes % (SIDE ** 3)
    axes = (ep % SIDE, (ep // SIDE) % SIDE, ep // (SIDE * SIDE))
    first = []
    for color in range(COLORS):
        d1, d2, d3 = (axes[(color + i) % 3] for i in range(3))
        block = ((sub * SIDE + d1) * SIDE + d2) * SIDE + d3
        first.append((color * rows + block * PART - color * PART).astype(jnp.float32))
    excess = jnp.maximum(count - BASE, 0.0)
    strict = ones_where(iota((n_experts, n_experts), 0) < iota((n_experts, n_experts), 1))
    ahead = dot(jnp.broadcast_to(excess, (8, n_experts)).astype(jnp.bfloat16), strict)[0:1, :]
    total = jnp.sum(excess, axis=1, keepdims=True)
    nowhere = 4.0 * COLORS * rows

    def places(member, rank):
        base = jnp.where(rank < PART, first[0], jnp.where(rank < 2 * PART, first[1], first[2]))
        late = ahead + (rank - BASE)
        place = jnp.where(rank < BASE, base + rank, jnp.where(late < OVER, COLORS * rows + late, nowhere))
        return jnp.sum(jnp.where(member, place, 0.0), axis=1, keepdims=True)

    pos0, pos1 = places(member0, rank0), places(member1, rank1)
    pos_ref[...] = jnp.concatenate([pos0, pos1], axis=1).astype(jnp.int32)
    row0, row1 = as_row(pos0), as_row(pos1)

    def block(i, carry):
        place = (iota((TILE, tok), 0) + i * TILE).astype(jnp.float32)
        pick = ones_where((place == row0) | (place == row1))
        got = dot(pick, x_ref[...]).astype(jnp.bfloat16)
        half = rows // TILE
        send_ref[i // half, pl.ds((i % half) * (TILE // PART), TILE // PART)] = got.reshape(TILE // PART, PART, dim)
        return carry

    lax.fori_loop(0, COLORS * rows // TILE, block, 0)
    place = (iota((32, tok), 0) + COLORS * rows).astype(jnp.float32)
    pick0, pick1 = ones_where(place == row0), ones_where(place == row1)
    got = dot(pick0 + pick1, x_ref[...]).astype(jnp.bfloat16)
    expert0 = jnp.broadcast_to(route_ref[:, 0:1] + 1, (tok, TAIL)).astype(jnp.bfloat16)
    expert1 = jnp.broadcast_to(route_ref[:, 1:2] + 1, (tok, TAIL)).astype(jnp.bfloat16)
    owner = dot(pick0, expert0) + dot(pick1, expert1)
    flag = jnp.where(total > OVER, 1.0, 0.0)
    tail = jnp.where(iota((32, TAIL), 1) == 0, owner, flag).astype(jnp.bfloat16)
    for color in range(COLORS):
        part = slice(color * SPARE, (color + 1) * SPARE)
        over_ref[color, :, 0:dim] = got[part, :]
        over_ref[color, :, dim:dim + TAIL] = tail[part, :]


class Torus:
    def __init__(self):
        self.sub = lax.axis_index("sub")
        ep = lax.axis_index("ep")
        self.at = (ep % SIDE, (ep // SIDE) % SIDE, ep // (SIDE * SIDE))

    def coord(self, axis, step):
        return (self.at[axis] + step) % SIDE

    def device(self, axis, step, core=0):
        at = list(self.at)
        at[axis] = self.coord(axis, step)
        return {"sub": (self.sub + core) % 2, "ep": (at[2] * SIDE + at[1]) * SIDE + at[0]}

    def greet(self):
        barrier = pltpu.get_barrier_semaphore()
        peers = [self.device(0, 0, 1)]
        for axis in range(3):
            for step in range(1, SIDE):
                for core in range(2):
                    peers.append(self.device(axis, step, core))
        for peer in peers:
            pl.semaphore_signal(barrier, inc=1, device_id=peer, device_id_type=MESH)
        pl.semaphore_wait(barrier, len(peers))


def remote(src, dst, send_sem, recv_sem, device):
    copy = pltpu.make_async_remote_copy(
        src_ref=src, dst_ref=dst, send_sem=send_sem, recv_sem=recv_sem, device_id=device, device_id_type=MESH)
    copy.start()
    return copy


def local(src, dst, sem):
    copy = pltpu.make_async_copy(src, dst, sem)
    copy.start()
    return copy


def arrive(copies):
    for copy in copies:
        copy.wait_recv()


def settle(copies):
    for copy in copies:
        if copy.is_remote:
            copy.wait_send()


def out_kernel(a, over, d, every, b, c, send, recv, here, esend, erecv, ehere):
    t = Torus()
    t.greet()
    s = t.sub
    done = []

    def hop(phase, k):
        ax = (k + phase) % 3
        c1, c2, c3 = (t.at[(k + i) % 3] for i in range(3))
        copies = []
        if phase == 0:
            mine = every.at[s, k, c1, c2, c3]
            copies.append(local(over.at[k], mine, ehere.at[k]))
            for step in (1, 3, 2):
                copies.append(remote(over.at[k], mine, esend.at[phase, k, step], erecv.at[phase, k, step], t.device(ax, step)))
        elif phase == 1:
            part = every.at[s, k, :, c2, c3]
            for step in (1, 3, 2):
                copies.append(remote(part, part, esend.at[phase, k, step], erecv.at[phase, k, step], t.device(ax, step)))
        else:
            part = every.at[s, k, :, :, c3]
            for step in (1, 3, 2):
                copies.append(remote(part, part, esend.at[phase, k, step], erecv.at[phase, k, step], t.device(ax, step)))
        for step in (1, 3, 2, 0):
            to = t.coord(ax, step)
            if phase == 0:
                for core in range(2):
                    src, dst = a.at[k, (s + core) % 2, to], b.at[k, s, c1]
                    if step == 0 and core == 0:
                        copies.append(local(src, dst, here.at[phase, k]))
                    else:
                        copies.append(remote(src, dst, send.at[phase, k, 2 * step + core], recv.at[phase, k, 2 * step + core], t.device(ax, step, core)))
            else:
                src, dst = (b.at[k, :, :, to], c.at[k, c2]) if phase == 1 else (c.at[k, :, :, :, to], d.at[k, c3])
                if step == 0:
                    copies.append(local(src, dst, here.at[phase, k]))
                else:
                    copies.append(remote(src, dst, send.at[phase, k, 2 * step], recv.at[phase, k, 2 * step], t.device(ax, step)))
        done.extend(copies)
        return copies

    flight = [hop(0, k) for k in range(COLORS)]
    for phase in range(1, 3):
        for k in range(COLORS):
            arrive(flight[k])
            flight[k] = hop(phase, k)
    for k in range(COLORS):
        arrive(flight[k])
        part = every.at[s, k]
        flight[k] = [remote(part, part, esend.at[3, k, 0], erecv.at[3, k, 0], t.device(0, 0, 1))]
        done.extend(flight[k])
    for k in range(COLORS):
        arrive(flight[k])
    settle(done)


def back_kernel(d, every, a, over, b, c, stage, sum3, sum2, sum1, got3, got2, got1,
                send, recv, here, esend, erecv):
    t = Torus()
    t.greet()
    s = t.sub
    done = []

    def hop(phase, k):
        ax = (k + phase) % 3
        c1, c2, c3 = (t.at[(k + i) % 3] for i in range(3))
        copies = []
        for step in (1, 3, 2, 0):
            to = t.coord(ax, step)
            if phase == 0:
                for core in range(2):
                    src, dst = b.at[k, (s + core) % 2, to], a.at[k, s, c1]
                    if step == 0 and core == 0:
                        copies.append(local(src, dst, here.at[phase, k]))
                    else:
                        copies.append(remote(src, dst, send.at[phase, k, 2 * step + core], recv.at[phase, k, 2 * step + core], t.device(ax, step, core)))
            else:
                src, dst = (c.at[k, to], b.at[k, :, :, c2]) if phase == 1 else (d.at[k, to], c.at[k, :, :, :, c3])
                if step == 0:
                    copies.append(local(src, dst, here.at[phase, k]))
                else:
                    copies.append(remote(src, dst, send.at[phase, k, 2 * step], recv.at[phase, k, 2 * step], t.device(ax, step)))
        done.extend(copies)
        return copies

    def spread(phase, k):
        ax = (k + phase) % 3
        copies = []
        for step in (1, 3, 2):
            to = t.coord(ax, step)
            src = (sum1.at[k, to], sum2.at[k, :, to], sum3.at[k, :, :, to])[phase]
            dst = (got1, got2, got3)[phase].at[k, SIDE - step - 1]
            copies.append(remote(src, dst, esend.at[phase, k, step], erecv.at[phase, k, step], t.device(ax, step)))
        done.extend(copies)
        return copies

    def gather(phase, k):
        mine = t.at[(k + phase) % 3]
        got = (got1, got2, got3)[phase]
        more = got[k, 0] + got[k, 1] + got[k, 2]
        if phase == 2:
            sum2[k] = sum3[k, :, :, mine] + more
        elif phase == 1:
            sum1[k] = sum2[k, :, mine] + more
        else:
            over[k] = sum1[k, mine] + more

    swap = []
    for k in range(COLORS):
        swap.append([remote(every.at[1 - s, k], stage.at[k], esend.at[3, k, 0], erecv.at[3, k, 0], t.device(0, 0, 1))])
        done.extend(swap[k])
    flight = [hop(2, k) for k in range(COLORS)]
    extra = [None] * COLORS
    for k in range(COLORS):
        arrive(swap[k])

        def add(i, carry, k=k):
            sum3[k, i] = every[s, k, i] + stage[k, i]
            return carry

        lax.fori_loop(0, SIDE, add, 0)
    for k in range(COLORS):
        extra[k] = spread(2, k)
    for phase in (1, 0):
        for k in range(COLORS):
            arrive(flight[k])
            flight[k] = hop(phase, k)
        for k in range(COLORS):
            arrive(extra[k])
            gather(phase + 1, k)
        for k in range(COLORS):
            extra[k] = spread(phase, k)
    for k in range(COLORS):
        arrive(extra[k])
        gather(0, k)
    for k in range(COLORS):
        arrive(flight[k])
    settle(done)


def ffn_kernel(x_ref, wg_ref, wu_ref, wd_ref, o_ref):
    n, part, dim = x_ref.shape
    o_ref[...] = expert_ffn(x_ref[...].reshape(n * part, dim), wg_ref, wu_ref, wd_ref).reshape(n, part, dim)


def over_ffn_kernel(n_ep, x_ref, wg_ref, wu_ref, wd_ref, o_ref, flag_ref):
    n, part, width = x_ref.shape
    dim = o_ref.shape[2]
    me = (lax.axis_index("sub") * n_ep + lax.axis_index("ep") + 1).astype(jnp.float32)
    tail = x_ref[:, :, dim:width].reshape(n * part, width - dim).astype(jnp.float32)
    mine = tail[:, 0:1] == me

    @pl.when(pl.program_id(0) == 0)
    def _():
        flag_ref[...] = jnp.zeros_like(flag_ref)

    flag_ref[...] = jnp.maximum(flag_ref[...], jnp.max(tail[:, 1:2], axis=0, keepdims=True))
    any_mine = jnp.max(jnp.where(mine, 1.0, 0.0)) > 0.0

    @pl.when(any_mine)
    def _():
        rows = x_ref[:, :, 0:dim].reshape(n * part, dim)
        out = expert_ffn(rows, wg_ref, wu_ref, wd_ref)
        o_ref[...] = jnp.where(mine, out.astype(jnp.float32), 0.0).astype(jnp.bfloat16).reshape(n, part, dim)

    @pl.when(jnp.logical_not(any_mine))
    def _():
        o_ref[...] = jnp.zeros_like(o_ref)


def mix_kernel(main_ref, over_ref, pos_ref, gate_ref, y_ref, main, over):
    n, part, dim = main_ref.shape
    n_rows = n * part
    main[...] = main_ref[...].reshape(n_rows, dim)
    over[...] = jnp.zeros_like(over)
    for color in range(COLORS):
        over[color * SPARE:(color + 1) * SPARE, :] = over_ref[color]

    def block(i, carry):
        rows = pl.ds(pl.multiple_of(i * TILE, TILE), TILE)
        lanes = iota((TILE, n_rows), 1)
        more = iota((TILE, over.shape[0]), 1) + n_rows
        total = jnp.zeros((TILE, dim), jnp.float32)
        for slot in range(2):
            pos = pos_ref[rows, slot:slot + 1]
            got = dot(ones_where(pos == lanes), main[...]) + dot(ones_where(pos == more), over[...])
            total = total + gate_ref[rows, slot:slot + 1] * got
        y_ref[rows, :] = total.astype(jnp.bfloat16)
        return carry

    lax.fori_loop(0, y_ref.shape[0] // TILE, block, 0)


def solution(mesh):
    n_sub, n_ep = mesh.shape["sub"], mesh.shape["ep"]
    n_dev = n_sub * n_ep
    tok_spec = P(("dp", "sub", "ep"), None)
    expert_spec = P(("sub", "ep"), None, None)
    group = ("sub", "ep")
    vmem = pl.BlockSpec(memory_space=pltpu.VMEM)
    hbm = pl.BlockSpec(memory_space=pl.ANY)
    params = pltpu.CompilerParams(vmem_limit_bytes=VMEM_LIMIT)
    bf16 = jnp.bfloat16

    def shape(*dims):
        return jax.ShapeDtypeStruct(dims, bf16)

    def weights(dim, ff):
        return [
            pl.BlockSpec((dim, ff), lambda i: (0, 0)),
            pl.BlockSpec((dim, ff), lambda i: (0, 0)),
            pl.BlockSpec((ff, dim), lambda i: (0, 0)),
        ]

    def wide(x, route, gate, w_gate, w_up, w_down):
        tok, dim = x.shape
        ff = w_gate.shape[1]
        cap = min(tok, 8 * tok // n_dev)
        rows = n_dev * cap
        send, pos = pl.pallas_call(
            functools.partial(wide_pack_kernel, cap),
            out_shape=[shape(rows, dim), jax.ShapeDtypeStruct((tok, 2), jnp.int32)],
            in_specs=[vmem, vmem],
            out_specs=[vmem, vmem],
            compiler_params=params,
            name="wide_pack",
        )(route, x)
        got = lax.all_to_all(send.reshape(n_dev, cap, dim), group, 0, 0).reshape(rows, dim)
        block = pl.BlockSpec((TILE, dim), lambda i: (i, 0))
        out = pl.pallas_call(
            wide_ffn_kernel,
            out_shape=shape(rows, dim),
            grid=(rows // TILE,),
            in_specs=[block] + weights(dim, ff),
            out_specs=block,
            compiler_params=params,
            name="wide_ffn",
        )(got, w_gate, w_up, w_down)
        ret = lax.all_to_all(out.reshape(n_dev, cap, dim), group, 0, 0).reshape(rows, dim)
        return pl.pallas_call(
            wide_mix_kernel,
            out_shape=shape(tok, dim),
            in_specs=[vmem, vmem, vmem],
            out_specs=vmem,
            compiler_params=params,
            name="wide_mix",
        )(ret, pos, gate)

    def exchange_params(number):
        return pltpu.CompilerParams(collective_id=number, has_side_effects=True, vmem_limit_bytes=VMEM_LIMIT)

    cube = (SIDE, SIDE, SIDE)

    def device_step(x, route, gate, w_gate, w_up, w_down):
        tok, dim = x.shape
        ff = w_gate.shape[2]
        w_gate, w_up, w_down = w_gate[0], w_up[0], w_down[0]
        main = (COLORS, 2) + cube + (PART, dim)
        late = (2, COLORS) + cube + (SPARE, dim + TAIL)
        sems = pltpu.SemaphoreType.DMA
        send, over, pos = pl.pallas_call(
            pack_kernel,
            out_shape=[shape(COLORS, n_dev, PART, dim), shape(COLORS, SPARE, dim + TAIL),
                       jax.ShapeDtypeStruct((tok, 2), jnp.int32)],
            in_specs=[vmem, vmem],
            out_specs=[vmem, vmem, vmem],
            compiler_params=params,
            name="pack",
        )(route, x)
        got, late_in = pl.pallas_call(
            out_kernel,
            out_shape=[shape(COLORS, SIDE, SIDE, 2, SIDE, PART, dim), shape(*late)],
            in_specs=[vmem, vmem],
            out_specs=[vmem, vmem],
            scratch_shapes=[
                pltpu.VMEM((COLORS, 2, SIDE, SIDE, SIDE, PART, dim), bf16),
                pltpu.VMEM((COLORS, SIDE, 2, SIDE, SIDE, PART, dim), bf16),
                sems((3, COLORS, 2 * SIDE)), sems((3, COLORS, 2 * SIDE)), sems((3, COLORS)),
                sems((4, COLORS, SIDE)), sems((4, COLORS, SIDE)), sems((COLORS,)),
            ],
            compiler_params=exchange_params(0),
            name="exchange_out",
        )(send.reshape(main), over)
        blocks = COLORS * n_dev
        step = TILE // PART
        out = pl.pallas_call(
            ffn_kernel,
            out_shape=shape(blocks, PART, dim),
            grid=(blocks // step,),
            in_specs=[pl.BlockSpec((step, PART, dim), lambda i: (i, 0, 0))] + weights(dim, ff),
            out_specs=pl.BlockSpec((step, PART, dim), lambda i: (i, 0, 0)),
            compiler_params=params,
            name="ffn",
        )(got.reshape(blocks, PART, dim), w_gate, w_up, w_down)
        step = TILE // SPARE
        late_out, flag = pl.pallas_call(
            functools.partial(over_ffn_kernel, n_ep),
            out_shape=[shape(blocks, SPARE, dim), jax.ShapeDtypeStruct((1, 1), jnp.float32)],
            grid=(blocks // step,),
            in_specs=[pl.BlockSpec((step, SPARE, dim + TAIL), lambda i: (i, 0, 0))] + weights(dim, ff),
            out_specs=[pl.BlockSpec((step, SPARE, dim), lambda i: (i, 0, 0)), pl.BlockSpec((1, 1), lambda i: (0, 0))],
            compiler_params=params,
            name="over_ffn",
        )(late_in.reshape(blocks, SPARE, dim + TAIL), w_gate, w_up, w_down)
        ret, over_ret = pl.pallas_call(
            back_kernel,
            out_shape=[shape(*main), shape(COLORS, SPARE, dim)],
            in_specs=[vmem, vmem],
            out_specs=[vmem, vmem],
            scratch_shapes=[
                pltpu.VMEM((COLORS, 2, SIDE, SIDE, SIDE, PART, dim), bf16),
                pltpu.VMEM((COLORS, SIDE, 2, SIDE, SIDE, PART, dim), bf16),
                pltpu.VMEM((COLORS,) + cube + (SPARE, dim), bf16),
                pltpu.VMEM((COLORS,) + cube + (SPARE, dim), bf16),
                pltpu.VMEM((COLORS, SIDE, SIDE, SPARE, dim), bf16),
                pltpu.VMEM((COLORS, SIDE, SPARE, dim), bf16),
                pltpu.VMEM((COLORS, SIDE - 1, SIDE, SIDE, SPARE, dim), bf16),
                pltpu.VMEM((COLORS, SIDE - 1, SIDE, SPARE, dim), bf16),
                pltpu.VMEM((COLORS, SIDE - 1, SPARE, dim), bf16),
                sems((3, COLORS, 2 * SIDE)), sems((3, COLORS, 2 * SIDE)), sems((3, COLORS)),
                sems((4, COLORS, SIDE)), sems((4, COLORS, SIDE)),
            ],
            compiler_params=exchange_params(1),
            name="exchange_back",
        )(out.reshape((COLORS, SIDE, SIDE, 2, SIDE, PART, dim)), late_out.reshape(late[:-1] + (dim,)))
        y = pl.pallas_call(
            mix_kernel,
            out_shape=shape(tok, dim),
            in_specs=[vmem] * 4,
            out_specs=vmem,
            scratch_shapes=[pltpu.VMEM((blocks * PART, dim), bf16), pltpu.VMEM((128, dim), bf16)],
            compiler_params=params,
            name="mix",
        )(ret.reshape(blocks, PART, dim), over_ret, pos, gate)
        return lax.cond(flag[0, 0] > 0.0, wide, lambda *args: y, x, route, gate, w_gate, w_up, w_down)

    return jax.shard_map(
        device_step,
        mesh=mesh,
        in_specs=(tok_spec, tok_spec, tok_spec, expert_spec, expert_spec, expert_spec),
        out_specs=tok_spec,
        check_vma=False,
    )
```

time: 327 us -> 186 us (0.57); the launches traced: 323 us -> 186 us
  Pallas kernels: 47.2 us -> 183 us
  waiting for transfers between devices: 132 us -> 0 us
  blocking collectives: 130 us -> 0 us
  starting transfers between devices: 11.1 us -> 0 us
    pallas_call x3 -> x6, Pallas kernels: 47.2 us -> 183 us  [the longest x1 80.3 us: device_step(): pl.pallas_call(out_kernel, out_shape=[shape(COLORS, SIDE, SIDE, 2, SIDE,...]
    all_to_all x1 -> x0, waiting for transfers between devices: 132 us -> none  [device_step(): lax.all_to_all(out.reshape(n_dev, cap, dim), group, 0, 0).reshape(rows, dim)]
    all_to_all x1 -> x0, blocking collectives: 130 us -> none  [device_step(): lax.all_to_all(send.reshape(n_dev, cap, dim), group, 0, 0)]
    all_to_all x1 -> x0, starting transfers between devices: 11.1 us -> none  [device_step(): lax.all_to_all(out.reshape(n_dev, cap, dim), group, 0, 0).reshape(rows, dim)]
  transfers between devices with their start and end apart: 1 -> 0, of which waited for: 1 -> 0; matrix products, arithmetic and copies ran while one was open for 0% -> 0% of each run, Pallas kernels for 0% -> 0%
where the time goes in v2:
time: 186 us
  Pallas kernels  183 us (98%)
  local copies, waits for them, and re-layouts  2.42 us (1%)
    pallas_call x1, Pallas kernels, device_step(): pl.pallas_call(out_kernel, out_shape=[shape(COLORS, SIDE, SIDE, 2, SIDE,...  80.3 us
    pallas_call x1, Pallas kernels, device_step(): pl.pallas_call(back_kernel, out_shape=[shape(*main), shape(COLORS, SPARE,...  67.5 us
    pallas_call x1, Pallas kernels, device_step(): pl.pallas_call(functools.partial(over_ffn_kernel, n_ep), out_shape=[shape...  11.4 us
    pallas_call x1, Pallas kernels, device_step(): pl.pallas_call(ffn_kernel, out_shape=shape(blocks, PART, dim), grid=(bloc...  8.66 us
    pallas_call x1, Pallas kernels, device_step(): pl.pallas_call(mix_kernel, out_shape=shape(tok, dim), in_specs=[vmem] * 4...  7.56 us
    pallas_call x1, Pallas kernels, device_step(): pl.pallas_call(pack_kernel, out_shape=[shape(COLORS, n_dev, PART, dim), s...  7 us

profile of v2, /device:TPU:1, one launch (start us, length us, event | category | flops | bytes accessed | tf_op | source)
XLA Modules:
  0.0 186.0 jit_solution(13222797104560863052)
XLA Ops:
  0.0 1.5 copy.9.route_ref
  1.5 0.0 copy-start
  1.5 0.0 copy-start.1
  1.5 0.0 copy-start.2
  1.5 7.0 %pack.1 = (bf16[3,128,4,1024]{3,2,1,0:T(4,128)(2,1)}, bf16[3,8,1152]{2,1,0:T(8,128)(2,1)}, s32[512,2]{1,0:T(8,128)}) custom-call(s32[512,2]{1,0:T(8,128)} %copy.9.route_ref, bf16[512,1024]{1,0:T(8,128)(2,1)} %x_ref.1), custom_call_target="tpu_custom_call" | custom-call | tf_op jit(solution)/shard_map/pack/pallas_call | solution.py:455
  8.6 80.3 %exchange_out.1 = (bf16[3,4,4,2,4,4,1024]{6,5,4,3,2,1,0:T(4,128)(2,1)}, bf16[2,3,4,4,4,8,1152]{6,5,4,3,2,1,0:T(8,128)(2,1)}) custom-call(bf16[3,2,4,4,4,4,1024]{6,5,4,3,2,1,0:T(4,128)(2,1)} %bitcast.30, bf16[3,8,1152]{2,1,0:T(8,128)(2,1)} %get-tuple-element.39.over), custom_call_target="tpu_custom_call" | custom-call | tf_op jit(solution)/shard_map/exchange_out/pallas_call | solution.py:464
  88.9 11.4 %over_ffn.1 = (bf16[384,8,1024]{2,1,0:T(8,128)(2,1)}, f32[1,1]{1,0:T(1,128)}) custom-call(bf16[384,8,1152]{2,1,0:T(8,128)(2,1)} %bitcast.27, bf16[1024,512]{1,0:T(8,128)(2,1)} %bitcast.17, bf16[1024,512]{1,0:T(8,128)(2,1)} %bitcast.20, bf16[512,1024]{1,0:T(8,128)(2,1)} %bitcast.23), custom_call_target="tpu_custom_call" | custom-call | tf_op jit(solution)/shard_map/over_ffn/pallas_call | solution.py:490
  100.3 0.0 copy-done
  100.3 0.0 copy-done.1
  100.3 0.0 copy-done.2
  100.4 8.7 %ffn.1 = bf16[384,4,1024]{2,1,0:T(4,128)(2,1)} custom-call(bf16[384,4,1024]{2,1,0:T(4,128)(2,1)} %bitcast.31, bf16[1024,512]{1,0:T(8,128)(2,1)S(1)} %bitcast.18, bf16[1024,512]{1,0:T(8,128)(2,1)S(1)} %bitcast.21, bf16[512,1024]{1,0:T(8,128)(2,1)S(1)} %bitcast.24), custom_call_target="tpu_custom_call" | custom-call | tf_op jit(solution)/shard_map/ffn/pallas_call | solution.py:480
  109.0 0.0 copy-start.4
  109.0 0.0 copy-start.3
  109.0 67.5 %exchange_back.1 = (bf16[3,2,4,4,4,4,1024]{6,5,4,3,2,1,0:T(4,128)(2,1)}, bf16[3,8,1024]{2,1,0:T(8,128)(2,1)}) custom-call(bf16[3,4,4,2,4,4,1024]{6,5,4,3,2,1,0:T(4,128)(2,1)} %bitcast.16, bf16[2,3,4,4,4,8,1024]{6,5,4,3,2,1,0:T(8,128)(2,1)} %bitcast.28), custom_call_target="tpu_custom_call" | custom-call | tf_op jit(solution)/shard_map/exchange_back/pallas_call | solution.py:499
  176.6 0.0 copy-done.4
  176.6 0.9 copy.10.gate_ref
  177.4 7.6 %mix.1 = bf16[512,1024]{1,0:T(8,128)(2,1)} custom-call(bf16[384,4,1024]{2,1,0:T(4,128)(2,1)} %bitcast.29, bf16[3,8,1024]{2,1,0:T(8,128)(2,1)} %get-tuple-element.45.over_ref, s32[512,2]{1,0:T(8,128)} %get-tuple-element.46.pos_ref, f32[512,2]{1,0:T(8,128)} %copy.10.gate_ref), custom_call_target="tpu_custom_call" | custom-call | tf_op jit(solution)/shard_map/mix/pallas_call | solution.py:520
  185.6 0.0 copy-done.3
  185.6 0.2 conditional.1
Async XLA Ops:
  1.5 98.8 %copy-start = (bf16[1,1024,512]{2,1,0:T(8,128)(2,1)S(1)}, bf16[1,1024,512]{2,1,0:T(8,128)(2,1)}, u32[]{:S(2)}) copy-start(bf16[1,1024,512]{2,1,0:T(8,128)(2,1)} %param.11) | copy-start | bytes 3145732
  1.5 98.8 %copy-start.1 = (bf16[1,1024,512]{2,1,0:T(8,128)(2,1)S(1)}, bf16[1,1024,512]{2,1,0:T(8,128)(2,1)}, u32[]{:S(2)}) copy-start(bf16[1,1024,512]{2,1,0:T(8,128)(2,1)} %param.12) | copy-start | bytes 3145732
  1.5 98.8 %copy-start.2 = (bf16[1,512,1024]{2,1,0:T(8,128)(2,1)S(1)}, bf16[1,512,1024]{2,1,0:T(8,128)(2,1)}, u32[]{:S(2)}) copy-start(bf16[1,512,1024]{2,1,0:T(8,128)(2,1)} %param.13) | copy-start | bytes 3145732
  109.0 67.5 %copy-start.4 = (f32[512,2]{0,1:T(2,128)S(1)}, f32[512,2]{0,1:T(2,128)}, u32[]{:S(2)}) copy-start(f32[512,2]{0,1:T(2,128)} %param.10) | copy-start | bytes 12292
  109.0 76.6 %copy-start.3 = (s32[512,2]{0,1:T(2,128)S(1)}, s32[512,2]{0,1:T(2,128)}, u32[]{:S(2)}) copy-start(s32[512,2]{0,1:T(2,128)} %param.9) | copy-start | bytes 12292

commit v3 on v1

v3 whole, which is shorter than its diff:
```python
import functools

import jax
import jax.numpy as jnp
from jax import lax
from jax.experimental import pallas as pl
from jax.experimental.pallas import tpu as pltpu
from jax.sharding import PartitionSpec as P

MESH = pl.DeviceIdType.MESH
TILE = 256
VMEM_LIMIT = 60 * 1024 * 1024
COLORS = 3
PART = 4
BASE = COLORS * PART
SPARE = 8
OVER = COLORS * SPARE
SIDE = 4
TAIL = 128


def iota(shape, dim):
    return lax.broadcasted_iota(jnp.int32, shape, dim)


def ones_where(mask):
    return jnp.where(mask, 1.0, 0.0).astype(jnp.bfloat16)


def dot(a, b):
    return jnp.dot(a, b, preferred_element_type=jnp.float32)


def expert_ffn(rows, wg_ref, wu_ref, wd_ref):
    act_a = dot(rows, wg_ref[...])
    act_b = dot(rows, wu_ref[...])
    hidden = (jax.nn.silu(act_a) * act_b).astype(jnp.bfloat16)
    return dot(hidden, wd_ref[...]).astype(jnp.bfloat16)


def ranks(route_ref, n_experts):
    tok = route_ref.shape[0]
    lanes = iota((tok, n_experts), 1)
    member0 = route_ref[:, 0:1] == lanes
    member1 = route_ref[:, 1:2] == lanes
    lower = ones_where(iota((tok, tok), 0) >= iota((tok, tok), 1))
    rank0 = dot(lower, ones_where(member0))
    rank1 = dot(lower, ones_where(member1)) + rank0[tok - 1:tok, :]
    return member0, member1, rank0 - 1.0, rank1 - 1.0, rank1[tok - 1:tok, :]


def as_row(column):
    return jnp.transpose(jnp.broadcast_to(column, (column.shape[0], 128)))[0:1, :]


def wide_pack_kernel(cap, route_ref, x_ref, send_ref, pos_ref):
    tok = x_ref.shape[0]
    rows = send_ref.shape[0]
    member0, member1, rank0, rank1, _ = ranks(route_ref, rows // cap)
    base = (iota(member0.shape, 1) * cap).astype(jnp.float32)
    pos0 = jnp.sum(jnp.where(member0, rank0 + base, 0.0), axis=1, keepdims=True)
    pos1 = jnp.sum(jnp.where(member1, rank1 + base, 0.0), axis=1, keepdims=True)
    pos_ref[...] = jnp.concatenate([pos0, pos1], axis=1).astype(jnp.int32)
    row0, row1 = as_row(pos0), as_row(pos1)

    def block(i, carry):
        place = (iota((TILE, tok), 0) + i * TILE).astype(jnp.float32)
        pick = ones_where((place == row0) | (place == row1))
        send_ref[pl.ds(pl.multiple_of(i * TILE, TILE), TILE), :] = dot(pick, x_ref[...]).astype(jnp.bfloat16)
        return carry

    lax.fori_loop(0, rows // TILE, block, 0)


def wide_ffn_kernel(x_ref, wg_ref, wu_ref, wd_ref, o_ref):
    o_ref[...] = expert_ffn(x_ref[...], wg_ref, wu_ref, wd_ref)


def wide_mix_kernel(ret_ref, pos_ref, gate_ref, y_ref):
    n_rows = ret_ref.shape[0]

    def block(i, carry):
        part = pl.ds(pl.multiple_of(i * TILE, TILE), TILE)
        lanes = iota((TILE, n_rows), 1)
        total = gate_ref[part, 0:1] * dot(ones_where(pos_ref[part, 0:1] == lanes), ret_ref[...])
        total = total + gate_ref[part, 1:2] * dot(ones_where(pos_ref[part, 1:2] == lanes), ret_ref[...])
        y_ref[part, :] = total.astype(jnp.bfloat16)
        return carry

    lax.fori_loop(0, y_ref.shape[0] // TILE, block, 0)


class Torus:
    def __init__(self):
        self.sub = lax.axis_index("sub")
        ep = lax.axis_index("ep")
        self.at = (ep % SIDE, (ep // SIDE) % SIDE, ep // (SIDE * SIDE))

    def coord(self, axis, step):
        return (self.at[axis] + step) % SIDE

    def device(self, axis, step, core=0):
        at = list(self.at)
        at[axis] = self.coord(axis, step)
        return {"sub": (self.sub + core) % 2, "ep": (at[2] * SIDE + at[1]) * SIDE + at[0]}

    def greet(self):
        barrier = pltpu.get_barrier_semaphore()
        peers = [self.device(0, 0, 1)]
        for axis in range(3):
            for step in range(1, SIDE):
                for core in range(2):
                    peers.append(self.device(axis, step, core))
        for peer in peers:
            pl.semaphore_signal(barrier, inc=1, device_id=peer, device_id_type=MESH)
        pl.semaphore_wait(barrier, len(peers))


def remote(src, dst, send_sem, recv_sem, device):
    return pltpu.make_async_remote_copy(
        src_ref=src, dst_ref=dst, send_sem=send_sem, recv_sem=recv_sem, device_id=device, device_id_type=MESH)


def start(copies):
    for copy in copies:
        copy.start()


def arrive(copies):
    for copy in copies:
        copy.wait_recv()


def settle(copies):
    for copy in copies:
        if copy.is_remote:
            copy.wait_send()


def at(i, table):
    for j, steps in table.items():
        @pl.when(i == j)
        def _(steps=steps):
            for step in steps:
                step()


STEPS = (1, 3, 2)
CHUNKS = [(k, h) for h in range(2) for k in range(COLORS)]


def layer_kernel(route_ref, gate_ref, x_ref, wg_hbm, wu_hbm, wd_hbm, y_ref, flag_ref,
                 wg, wu, wd, a, b, c, d, cc, bb, aa, over, every, late, stage, sum2, sum1, got3, got2, got1, last,
                 pos, total, send, recv, bsend, brecv, esend, erecv, rsend, rrecv, here, wsem):
    tok, dim = x_ref.shape
    rows = 2 * SIDE ** 3 * PART
    t = Torus()
    s = t.sub
    load = [pltpu.make_async_copy(src, dst, wsem.at[i])
            for i, (src, dst) in enumerate(((wg_hbm, wg), (wu_hbm, wu), (wd_hbm, wd)))]
    start(load)
    t.greet()

    def place(k):
        return tuple(t.at[(k + i) % 3] for i in range(3))

    def out(phase, k, h):
        ax, sh = (k + phase) % 3, (s + h) % 2
        c1, c2, c3 = place(k)
        copies = []
        for step in STEPS + (0,):
            to = t.coord(ax, step)
            core = h if phase == 0 else 0
            if phase == 0:
                src, dst = a.at[k, sh, to], b.at[k, s, c1]
            elif phase == 1:
                src, dst = b.at[k, sh, :, to], c.at[k, sh, c2]
            else:
                src, dst = c.at[k, sh, :, :, to], d.at[k, sh, c3]
            if step == 0 and core == 0:
                copies.append(pltpu.make_async_copy(src, dst, recv.at[phase, k, h, step]))
            else:
                copies.append(remote(src, dst, send.at[phase, k, h, step], recv.at[phase, k, h, step],
                                     t.device(ax, step, core)))
        return copies

    def back(phase, k, h):
        ax, sh = (k + phase) % 3, (s + h) % 2
        c1, c2, c3 = place(k)
        copies = []
        for step in STEPS + (0,):
            to = t.coord(ax, step)
            core = h if phase == 0 else 0
            if phase == 0:
                src, dst = bb.at[k, sh, to], aa.at[k, s, c1]
            elif phase == 1:
                src, dst = cc.at[k, sh, to], bb.at[k, sh, :, c2]
            else:
                src, dst = d.at[k, sh, to], cc.at[k, sh, :, :, c3]
            if step == 0 and core == 0:
                copies.append(pltpu.make_async_copy(src, dst, brecv.at[phase, k, h, step]))
            else:
                copies.append(remote(src, dst, bsend.at[phase, k, h, step], brecv.at[phase, k, h, step],
                                     t.device(ax, step, core)))
        return copies

    def gather(phase, k):
        c1, c2, c3 = place(k)
        if phase == 3:
            part = every.at[s, k]
            return [remote(part, part, esend.at[3, k, 0], erecv.at[3, k, 0], t.device(0, 0, 1))]
        mine = (every.at[s, k, c1, c2, c3], every.at[s, k, :, c2, c3], every.at[s, k, :, :, c3])[phase]
        copies = [remote(mine, mine, esend.at[phase, k, step], erecv.at[phase, k, step],
                         t.device((k + phase) % 3, step)) for step in STEPS]
        return copies

    def reduce(phase, k):
        if phase == 3:
            return [remote(late.at[1 - s, k], stage.at[k], rsend.at[3, k, 0], rrecv.at[3, k, 0], t.device(0, 0, 1))]
        copies = []
        for step in STEPS:
            to = t.coord((k + phase) % 3, step)
            src = (sum1.at[k, to], sum2.at[k, :, to], late.at[s, k, :, :, to])[phase]
            dst = (got1, got2, got3)[phase].at[k, SIDE - step - 1]
            copies.append(remote(src, dst, rsend.at[phase, k, step], rrecv.at[phase, k, step],
                                 t.device((k + phase) % 3, step)))
        return copies

    def merge(phase, k):
        if phase == 3:
            def add(i, carry):
                late[s, k, i] = late[s, k, i] + stage[k, i]
                return carry

            lax.fori_loop(0, SIDE, add, 0)
            return
        mine = t.at[(k + phase) % 3]
        got = (got1, got2, got3)[phase]
        more = got[k, 0] + got[k, 1] + got[k, 2]
        if phase == 2:
            sum2[k] = late[s, k, :, :, mine] + more
        elif phase == 1:
            sum1[k] = sum2[k, :, mine] + more
        else:
            last[k * SPARE:(k + 1) * SPARE, :] = sum1[k, mine] + more

    n_experts = 2 * SIDE ** 3
    member0, member1, rank0, rank1, count = ranks(route_ref, n_experts)
    lanes = iota((1, n_experts), 1)
    sub, ep = lanes // (SIDE ** 3), lanes % (SIDE ** 3)
    axes = (ep % SIDE, (ep // SIDE) % SIDE, ep // (SIDE * SIDE))
    first = []
    for k in range(COLORS):
        d1, d2, d3 = (axes[(k + i) % 3] for i in range(3))
        block = ((sub * SIDE + d1) * SIDE + d2) * SIDE + d3
        first.append((k * rows + block * PART - k * PART).astype(jnp.float32))
    excess = jnp.maximum(count - BASE, 0.0)
    strict = ones_where(iota((n_experts, n_experts), 0) < iota((n_experts, n_experts), 1))
    ahead = dot(jnp.broadcast_to(excess, (8, n_experts)).astype(jnp.bfloat16), strict)[0:1, :]
    n_over = jnp.sum(excess, axis=1, keepdims=True)
    nowhere = 4.0 * COLORS * rows

    def places(member, rank):
        base = jnp.where(rank < PART, first[0], jnp.where(rank < 2 * PART, first[1], first[2]))
        behind = ahead + (rank - BASE)
        where = jnp.where(rank < BASE, base + rank, jnp.where(behind < OVER, COLORS * rows + behind, nowhere))
        return jnp.sum(jnp.where(member, where, 0.0), axis=1, keepdims=True)

    pos0, pos1 = places(member0, rank0), places(member1, rank1)
    pos[:, 0:1] = pos0.astype(jnp.int32)
    pos[:, 1:2] = pos1.astype(jnp.int32)
    row0, row1 = as_row(pos0), as_row(pos1)

    spot = (iota((32, tok), 0) + COLORS * rows).astype(jnp.float32)
    pick0, pick1 = ones_where(spot == row0), ones_where(spot == row1)
    got = dot(pick0 + pick1, x_ref[...]).astype(jnp.bfloat16)
    expert0 = jnp.broadcast_to(route_ref[:, 0:1] + 1, (tok, TAIL)).astype(jnp.bfloat16)
    expert1 = jnp.broadcast_to(route_ref[:, 1:2] + 1, (tok, TAIL)).astype(jnp.bfloat16)
    owner = dot(pick0, expert0) + dot(pick1, expert1)
    flag = jnp.where(n_over > OVER, 1.0, 0.0)
    tail = jnp.where(iota((32, TAIL), 1) == 0, owner, flag).astype(jnp.bfloat16)
    for k in range(COLORS):
        c1, c2, c3 = place(k)
        part = slice(k * SPARE, (k + 1) * SPARE)
        every[s, k, c1, c2, c3, :, 0:dim] = got[part, :]
        every[s, k, c1, c2, c3, :, dim:dim + TAIL] = tail[part, :]

    half = rows // TILE

    def pack(i, carry):
        spot = (iota((TILE, tok), 0) + i * TILE).astype(jnp.float32)
        pick = ones_where((spot == row0) | (spot == row1))
        got = dot(pick, x_ref[...]).astype(jnp.bfloat16)
        a[i // half, i % half] = got.reshape(SIDE, SIDE, SIDE, PART, dim)
        at(i, {
            2: [lambda: start(out(0, 0, 0)), lambda: start(out(0, 0, 1))],
            4: [lambda: start(out(0, 1, 0)), lambda: start(out(0, 1, 1))],
        })
        return carry

    lax.fori_loop(0, COLORS * half, pack, 0)
    start(out(0, 2, 0) + out(0, 2, 1))
    for k in range(COLORS):
        start(gather(0, k))
    for phase in range(1, 3):
        for k, h in CHUNKS:
            arrive(out(phase - 1, k, h))
            start(out(phase, k, h))
        for k in range(COLORS):
            arrive(gather(phase - 1, k))
            start(gather(phase, k))
    arrive(load)

    def ffn(i, carry):
        k, h = i % COLORS, i // COLORS
        sh = (s + h) % 2
        at(i, {j: [lambda q=q: arrive(out(2, *q))] for j, q in enumerate(CHUNKS)})
        d[k, sh] = expert_ffn(d[k, sh].reshape(TILE, dim), wg, wu, wd).reshape(SIDE, SIDE, SIDE, PART, dim)
        at(i, {j: [lambda q=q: start(back(2, *q))] for j, q in enumerate(CHUNKS)})
        return carry

    lax.fori_loop(0, len(CHUNKS), ffn, 0)

    me = (s * SIDE ** 3 + lax.axis_index("ep") + 1).astype(jnp.float32)
    flag_ref[...] = jnp.zeros_like(flag_ref)
    order = [2, 4, 5, 7, 9, 10]

    def over_ffn(i, carry):
        core, k, part = (s + i // 6) % 2, (i // 2) % COLORS, (i % 2) * 2
        before = {j: [lambda j=j: arrive(gather(2, j)), lambda j=j: start(gather(3, j))] for j in range(COLORS)}
        before.update({6 + 2 * j: [lambda j=j: arrive(gather(3, j))] for j in range(COLORS)})
        at(i, before)
        got = every[core, k, pl.ds(part, 2)].reshape(TILE, dim + TAIL)
        tail = got[:, dim:dim + TAIL].astype(jnp.float32)
        flag_ref[...] = jnp.maximum(flag_ref[...], jnp.max(tail[:, 1:2], axis=0, keepdims=True))
        result = expert_ffn(got[:, 0:dim], wg, wu, wd).astype(jnp.float32)
        result = jnp.where(tail[:, 0:1] == me, result, 0.0).astype(jnp.bfloat16)
        late[core, k, pl.ds(part, 2)] = result.reshape(2, SIDE, SIDE, SPARE, dim)
        at(i, {order[j]: [lambda q=q: arrive(back(2, *q)), lambda q=q: start(back(1, *q))]
               for j, q in enumerate(CHUNKS)})
        at(i, {8: [lambda: start(reduce(3, 0))]})
        return carry

    lax.fori_loop(0, 12, over_ffn, 0)
    start(reduce(3, 1))
    start(reduce(3, 2))
    for k in range(COLORS):
        arrive(reduce(3, k))
        merge(3, k)
        if k:
            start(reduce(2, k - 1))
    start(reduce(2, 2))
    for k, h in CHUNKS:
        arrive(back(1, k, h))
        start(back(0, k, h))
    for phase in (2, 1):
        for k in range(COLORS):
            arrive(reduce(phase, k))
            merge(phase, k)
            if k:
                start(reduce(phase - 1, k - 1))
        start(reduce(phase - 1, 2))
    total[...] = jnp.zeros_like(total)

    def mix(i, carry):
        at(i, {k: [lambda k=k: arrive(back(0, k, 0)), lambda k=k: arrive(back(0, k, 1))] for k in range(COLORS)})
        got = aa[i].reshape(rows, dim)
        lanes = iota((TILE, rows), 1) + i * rows
        for part in range(tok // TILE):
            where = pl.ds(part * TILE, TILE)
            for slot in range(2):
                pick = ones_where(pos[where, slot:slot + 1] == lanes)
                total[where, :] += gate_ref[where, slot:slot + 1] * dot(pick, got)
        return carry

    lax.fori_loop(0, COLORS, mix, 0)
    last[...] = jnp.zeros_like(last)
    for k in range(COLORS):
        arrive(reduce(0, k))
        merge(0, k)
    lanes = iota((tok, last.shape[0]), 1) + COLORS * rows
    more = jnp.zeros((tok, dim), jnp.float32)
    for slot in range(2):
        more = more + gate_ref[:, slot:slot + 1] * dot(ones_where(pos[:, slot:slot + 1] == lanes), last[...])
    y_ref[...] = (total[...] + more).astype(jnp.bfloat16)
    for k in range(COLORS):
        for phase in range(3):
            for h in range(2):
                settle(out(phase, k, h) + back(phase, k, h))
        for phase in range(4):
            settle(gather(phase, k) + reduce(phase, k))


def solution(mesh):
    n_sub, n_ep = mesh.shape["sub"], mesh.shape["ep"]
    n_dev = n_sub * n_ep
    tok_spec = P(("dp", "sub", "ep"), None)
    expert_spec = P(("sub", "ep"), None, None)
    group = ("sub", "ep")
    vmem = pl.BlockSpec(memory_space=pltpu.VMEM)
    hbm = pl.BlockSpec(memory_space=pl.ANY)
    params = pltpu.CompilerParams(vmem_limit_bytes=VMEM_LIMIT)
    bf16 = jnp.bfloat16

    def shape(*dims):
        return jax.ShapeDtypeStruct(dims, bf16)

    def weights(dim, ff):
        return [
            pl.BlockSpec((dim, ff), lambda i: (0, 0)),
            pl.BlockSpec((dim, ff), lambda i: (0, 0)),
            pl.BlockSpec((ff, dim), lambda i: (0, 0)),
        ]

    def wide(x, route, gate, w_gate, w_up, w_down):
        tok, dim = x.shape
        ff = w_gate.shape[1]
        cap = min(tok, 8 * tok // n_dev)
        rows = n_dev * cap
        send, pos = pl.pallas_call(
            functools.partial(wide_pack_kernel, cap),
            out_shape=[shape(rows, dim), jax.ShapeDtypeStruct((tok, 2), jnp.int32)],
            in_specs=[vmem, vmem],
            out_specs=[vmem, vmem],
            compiler_params=params,
            name="wide_pack",
        )(route, x)
        got = lax.all_to_all(send.reshape(n_dev, cap, dim), group, 0, 0).reshape(rows, dim)
        block = pl.BlockSpec((TILE, dim), lambda i: (i, 0))
        out = pl.pallas_call(
            wide_ffn_kernel,
            out_shape=shape(rows, dim),
            grid=(rows // TILE,),
            in_specs=[block] + weights(dim, ff),
            out_specs=block,
            compiler_params=params,
            name="wide_ffn",
        )(got, w_gate, w_up, w_down)
        ret = lax.all_to_all(out.reshape(n_dev, cap, dim), group, 0, 0).reshape(rows, dim)
        return pl.pallas_call(
            wide_mix_kernel,
            out_shape=shape(tok, dim),
            in_specs=[vmem, vmem, vmem],
            out_specs=vmem,
            compiler_params=params,
            name="wide_mix",
        )(ret, pos, gate)

    cube = (SIDE, SIDE, SIDE)

    def device_step(x, route, gate, w_gate, w_up, w_down):
        tok, dim = x.shape
        ff = w_gate.shape[2]
        w_gate, w_up, w_down = w_gate[0], w_up[0], w_down[0]
        sems = pltpu.SemaphoreType.DMA
        main = pltpu.VMEM((COLORS, 2) + cube + (PART, dim), bf16)
        pairs = sems((3, COLORS, 2, SIDE))
        quads = sems((4, COLORS, SIDE))
        y, flag = pl.pallas_call(
            layer_kernel,
            out_shape=[shape(tok, dim), jax.ShapeDtypeStruct((1, 1), jnp.float32)],
            in_specs=[vmem, vmem, vmem, hbm, hbm, hbm],
            out_specs=[vmem, vmem],
            scratch_shapes=[
                pltpu.VMEM((dim, ff), bf16), pltpu.VMEM((dim, ff), bf16), pltpu.VMEM((ff, dim), bf16),
                main, main, main, main, main, main, main,
                pltpu.VMEM((COLORS, SPARE, dim + TAIL), bf16),
                pltpu.VMEM((2, COLORS) + cube + (SPARE, dim + TAIL), bf16),
                pltpu.VMEM((2, COLORS) + cube + (SPARE, dim), bf16),
                pltpu.VMEM((COLORS,) + cube + (SPARE, dim), bf16),
                pltpu.VMEM((COLORS, SIDE, SIDE, SPARE, dim), bf16),
                pltpu.VMEM((COLORS, SIDE, SPARE, dim), bf16),
                pltpu.VMEM((COLORS, SIDE - 1, SIDE, SIDE, SPARE, dim), bf16),
                pltpu.VMEM((COLORS, SIDE - 1, SIDE, SPARE, dim), bf16),
                pltpu.VMEM((COLORS, SIDE - 1, SPARE, dim), bf16),
                pltpu.VMEM((128, dim), bf16),
                pltpu.VMEM((tok, 128), jnp.int32),
                pltpu.VMEM((tok, dim), jnp.float32),
                pairs, pairs, pairs, pairs, quads, quads, quads, quads, sems((3,)), sems((3,)),
            ],
            compiler_params=pltpu.CompilerParams(
                collective_id=0, has_side_effects=True, vmem_limit_bytes=67043328),
            name="layer",
        )(route, gate, x, w_gate, w_up, w_down)
        return lax.cond(flag[0, 0] > 0.0, wide, lambda *args: y, x, route, gate, w_gate, w_up, w_down)

    return jax.shard_map(
        device_step,
        mesh=mesh,
        in_specs=(tok_spec, tok_spec, tok_spec, expert_spec, expert_spec, expert_spec),
        out_specs=tok_spec,
        check_vma=False,
    )
```

time: 327 us -> 132 us (0.40); the launches traced: 323 us -> 132 us
  waiting for transfers between devices: 132 us -> 0 us
  blocking collectives: 130 us -> 0 us
  Pallas kernels: 47.2 us -> 126 us
  starting transfers between devices: 11.1 us -> 0 us
    all_to_all x1 -> x0, waiting for transfers between devices: 132 us -> none  [device_step(): lax.all_to_all(out.reshape(n_dev, cap, dim), group, 0, 0).reshape(rows, dim)]
    all_to_all x1 -> x0, blocking collectives: 130 us -> none  [device_step(): lax.all_to_all(send.reshape(n_dev, cap, dim), group, 0, 0)]
    pallas_call x3 -> x1, Pallas kernels: 47.2 us -> 126 us  [device_step(): pl.pallas_call(layer_kernel, out_shape=[shape(tok, dim), jax.ShapeDtypeSt...]
    all_to_all x1 -> x0, starting transfers between devices: 11.1 us -> none  [device_step(): lax.all_to_all(out.reshape(n_dev, cap, dim), group, 0, 0).reshape(rows, dim)]
  transfers between devices with their start and end apart: 1 -> 0, of which waited for: 1 -> 0; matrix products, arithmetic and copies ran while one was open for 0% -> 0% of each run, Pallas kernels for 0% -> 0%
where the time goes in v3:
time: 132 us
  Pallas kernels  126 us (95%)
  local copies, waits for them, and re-layouts  5.34 us (4%)
    pallas_call x1, Pallas kernels, device_step(): pl.pallas_call(layer_kernel, out_shape=[shape(tok, dim), jax.ShapeDtypeSt...  126 us
    unnamed x3, local copies, waits for them, and re-layouts  5.34 us

profile of v3, /device:TPU:1, one launch (start us, length us, event | category | flops | bytes accessed | tf_op | source)
XLA Modules:
  0.0 131.8 jit_solution(17978107772138422664)
XLA Ops:
  0.0 1.5 %copy.10.gate_ref = f32[512,2]{1,0:T(8,128)} copy(f32[512,2]{0,1:T(2,128)} %param.10) | data formatting | bytes 8192 | tf_op args[2]
  1.5 1.5 %copy.9.route_ref = s32[512,2]{1,0:T(8,128)} copy(s32[512,2]{0,1:T(2,128)} %param.9) | data formatting | bytes 8192 | tf_op args[1]
  3.1 125.5 %layer.1 = (bf16[512,1024]{1,0:T(8,128)(2,1)}, f32[1,1]{1,0:T(1,128)}) custom-call(s32[512,2]{1,0:T(8,128)} %copy.9.route_ref, f32[512,2]{1,0:T(8,128)} %copy.10.gate_ref, bf16[512,1024]{1,0:T(8,128)(2,1)} %x_ref.1, bf16[1024,512]{1,0:T(8,128)(2,1)} %bitcast.11, bf16[1024,512]{1,0:T(8,128)(2,1)} %bitcast.13, bf16[512,1024]{1,0:T(8,128)(2,1)} %bitcast.15), custom_call_target="tpu_custom_call" | custom-call | tf_op jit(solution)/shard_map/layer/pallas_call | solution.py:459
  129.3 0.2 conditional.1
  129.5 2.3 %copy.16 = bf16[512,1024]{1,0:T(8,128)(2,1)} copy(bf16[512,1024]{1,0:T(8,128)(2,1)} %get-tuple-element.33) | data formatting | bytes 2097152

commit v4 on v3

--- a/solution.py
+++ b/solution.py
@@ -38,11 +38,11 @@
     return dot(hidden, wd_ref[...]).astype(jnp.bfloat16)
 
 
-def ranks(route_ref, n_experts):
-    tok = route_ref.shape[0]
+def ranks(route0, route1, n_experts):
+    tok = route0.shape[0]
     lanes = iota((tok, n_experts), 1)
-    member0 = route_ref[:, 0:1] == lanes
-    member1 = route_ref[:, 1:2] == lanes
+    member0 = route0 == lanes
+    member1 = route1 == lanes
     lower = ones_where(iota((tok, tok), 0) >= iota((tok, tok), 1))
     rank0 = dot(lower, ones_where(member0))
     rank1 = dot(lower, ones_where(member1)) + rank0[tok - 1:tok, :]
@@ -56,7 +56,7 @@
 def wide_pack_kernel(cap, route_ref, x_ref, send_ref, pos_ref):
     tok = x_ref.shape[0]
     rows = send_ref.shape[0]
-    member0, member1, rank0, rank1, _ = ranks(route_ref, rows // cap)
+    member0, member1, rank0, rank1, _ = ranks(route_ref[:, 0:1], route_ref[:, 1:2], rows // cap)
     base = (iota(member0.shape, 1) * cap).astype(jnp.float32)
     pos0 = jnp.sum(jnp.where(member0, rank0 + base, 0.0), axis=1, keepdims=True)
     pos1 = jnp.sum(jnp.where(member1, rank1 + base, 0.0), axis=1, keepdims=True)
@@ -113,7 +113,7 @@
                     peers.append(self.device(axis, step, core))
         for peer in peers:
             pl.semaphore_signal(barrier, inc=1, device_id=peer, device_id_type=MESH)
-        pl.semaphore_wait(barrier, len(peers))
+        return lambda: pl.semaphore_wait(barrier, len(peers))
 
 
 def remote(src, dst, send_sem, recv_sem, device):
@@ -150,8 +150,8 @@
 
 
 def layer_kernel(route_ref, gate_ref, x_ref, wg_hbm, wu_hbm, wd_hbm, y_ref, flag_ref,
-                 wg, wu, wd, a, b, c, d, cc, bb, aa, over, every, late, stage, sum2, sum1, got3, got2, got1, last,
-                 pos, total, send, recv, bsend, brecv, esend, erecv, rsend, rrecv, here, wsem):
+                 wg, wu, wd, a, b, c, d, cc, bb, aa, every, late, stage, sum2, sum1, relay, got3, got2, got1, last,
+                 cols, total, send, recv, bsend, brecv, esend, erecv, rsend, rrecv, wsem):
     tok, dim = x_ref.shape
     rows = 2 * SIDE ** 3 * PART
     t = Torus()
@@ -159,7 +159,7 @@
     load = [pltpu.make_async_copy(src, dst, wsem.at[i])
             for i, (src, dst) in enumerate(((wg_hbm, wg), (wu_hbm, wu), (wd_hbm, wd)))]
     start(load)
-    t.greet()
+    everyone_here = t.greet()
 
     def place(k):
         return tuple(t.at[(k + i) % 3] for i in range(3))
@@ -209,19 +209,30 @@
         if phase == 3:
             part = every.at[s, k]
             return [remote(part, part, esend.at[3, k, 0], erecv.at[3, k, 0], t.device(0, 0, 1))]
+        if phase == 4:
+            copies = []
+            for step, part in ((1, slice(0, SIDE // 2)), (3, slice(SIDE // 2, SIDE))):
+                far = every.at[s, k, part, :, t.coord((k + 2) % 3, -step)]
+                copies.append(remote(far, far, esend.at[4, k, step], erecv.at[4, k, step], t.device((k + 2) % 3, step)))
+            return copies
         mine = (every.at[s, k, c1, c2, c3], every.at[s, k, :, c2, c3], every.at[s, k, :, :, c3])[phase]
-        copies = [remote(mine, mine, esend.at[phase, k, step], erecv.at[phase, k, step],
-                         t.device((k + phase) % 3, step)) for step in STEPS]
-        return copies
+        return [remote(mine, mine, esend.at[phase, k, step], erecv.at[phase, k, step],
+                       t.device((k + phase) % 3, step)) for step in (STEPS[:2] if phase == 2 else STEPS)]
 
     def reduce(phase, k):
         if phase == 3:
             return [remote(late.at[1 - s, k], stage.at[k], rsend.at[3, k, 0], rrecv.at[3, k, 0], t.device(0, 0, 1))]
         copies = []
-        for step in STEPS:
+        if phase == 4:
+            far = t.coord((k + 2) % 3, 2)
+            for i, (step, part) in enumerate(((1, slice(0, SIDE // 2)), (3, slice(SIDE // 2, SIDE)))):
+                copies.append(remote(late.at[s, k, part, :, far], relay.at[k, i], rsend.at[4, k, step],
+                                     rrecv.at[4, k, step], t.device((k + 2) % 3, step)))
+            return copies
+        for step in STEPS[:2] if phase == 2 else STEPS:
             to = t.coord((k + phase) % 3, step)
             src = (sum1.at[k, to], sum2.at[k, :, to], late.at[s, k, :, :, to])[phase]
-            dst = (got1, got2, got3)[phase].at[k, SIDE - step - 1]
+            dst = (got1, got2, got3)[phase].at[k, step // 2 if phase == 2 else step - 1]
             copies.append(remote(src, dst, rsend.at[phase, k, step], rrecv.at[phase, k, step],
                                  t.device((k + phase) % 3, step)))
         return copies
@@ -234,9 +245,16 @@
 
             lax.fori_loop(0, SIDE, add, 0)
             return
+        if phase == 4:
+            right, left = t.coord((k + 2) % 3, 1), t.coord((k + 2) % 3, 3)
+            late[s, k, 0:SIDE // 2, :, right] = late[s, k, 0:SIDE // 2, :, right] + relay[k, 0]
+            late[s, k, SIDE // 2:SIDE, :, left] = late[s, k, SIDE // 2:SIDE, :, left] + relay[k, 1]
+            return
         mine = t.at[(k + phase) % 3]
         got = (got1, got2, got3)[phase]
-        more = got[k, 0] + got[k, 1] + got[k, 2]
+        more = got[k, 0] + got[k, 1]
+        if phase < 2:
+            more = more + got[k, 2]
         if phase == 2:
             sum2[k] = late[s, k, :, :, mine] + more
         elif phase == 1:
@@ -245,7 +263,12 @@
             last[k * SPARE:(k + 1) * SPARE, :] = sum1[k, mine] + more
 
     n_experts = 2 * SIDE ** 3
-    member0, member1, rank0, rank1, count = ranks(route_ref, n_experts)
+    table = jnp.concatenate([route_ref[...].astype(jnp.float32), gate_ref[...], jnp.zeros((4, tok), jnp.float32)], axis=0)
+    table = jnp.transpose(table)
+    route0, route1 = table[:, 0:1].astype(jnp.int32), table[:, 1:2].astype(jnp.int32)
+    gates = slice(2, 4)
+    cols[:, gates] = table[:, gates]
+    member0, member1, rank0, rank1, count = ranks(route0, route1, n_experts)
     lanes = iota((1, n_experts), 1)
     sub, ep = lanes // (SIDE ** 3), lanes % (SIDE ** 3)
     axes = (ep % SIDE, (ep // SIDE) % SIDE, ep // (SIDE * SIDE))
@@ -267,15 +290,29 @@
         return jnp.sum(jnp.where(member, where, 0.0), axis=1, keepdims=True)
 
     pos0, pos1 = places(member0, rank0), places(member1, rank1)
-    pos[:, 0:1] = pos0.astype(jnp.int32)
-    pos[:, 1:2] = pos1.astype(jnp.int32)
-    row0, row1 = as_row(pos0), as_row(pos1)
+    cols[:, 0:1] = pos0
+    cols[:, 1:2] = pos1
+    both = jnp.transpose(jnp.where(iota((tok, 128), 1) == 0, pos0, pos1))
+    row0, row1 = both[0:1, :], both[1:2, :]
+
+    def pack(i, carry):
+        k, sh = i % COLORS, (s + i // COLORS) % 2
+        spot = (iota((TILE, tok), 0) + (k * rows + sh * TILE)).astype(jnp.float32)
+        pick = ones_where((spot == row0) | (spot == row1))
+        got = dot(pick, x_ref[...]).astype(jnp.bfloat16)
+        a[k, sh] = got.reshape(SIDE, SIDE, SIDE, PART, dim)
+        events = {j + 1: [lambda q=q: start(out(0, *q))] for j, q in enumerate(CHUNKS[:-1])}
+        events[1].insert(0, everyone_here)
+        at(i, events)
+        return carry
+
+    lax.fori_loop(0, len(CHUNKS), pack, 0)
 
     spot = (iota((32, tok), 0) + COLORS * rows).astype(jnp.float32)
     pick0, pick1 = ones_where(spot == row0), ones_where(spot == row1)
     got = dot(pick0 + pick1, x_ref[...]).astype(jnp.bfloat16)
-    expert0 = jnp.broadcast_to(route_ref[:, 0:1] + 1, (tok, TAIL)).astype(jnp.bfloat16)
-    expert1 = jnp.broadcast_to(route_ref[:, 1:2] + 1, (tok, TAIL)).astype(jnp.bfloat16)
+    expert0 = jnp.broadcast_to(route0 + 1, (tok, TAIL)).astype(jnp.bfloat16)
+    expert1 = jnp.broadcast_to(route1 + 1, (tok, TAIL)).astype(jnp.bfloat16)
     owner = dot(pick0, expert0) + dot(pick1, expert1)
     flag = jnp.where(n_over > OVER, 1.0, 0.0)
     tail = jnp.where(iota((32, TAIL), 1) == 0, owner, flag).astype(jnp.bfloat16)
@@ -284,22 +321,7 @@
         part = slice(k * SPARE, (k + 1) * SPARE)
         every[s, k, c1, c2, c3, :, 0:dim] = got[part, :]
         every[s, k, c1, c2, c3, :, dim:dim + TAIL] = tail[part, :]
-
-    half = rows // TILE
-
-    def pack(i, carry):
-        spot = (iota((TILE, tok), 0) + i * TILE).astype(jnp.float32)
-        pick = ones_where((spot == row0) | (spot == row1))
-        got = dot(pick, x_ref[...]).astype(jnp.bfloat16)
-        a[i // half, i % half] = got.reshape(SIDE, SIDE, SIDE, PART, dim)
-        at(i, {
-            2: [lambda: start(out(0, 0, 0)), lambda: start(out(0, 0, 1))],
-            4: [lambda: start(out(0, 1, 0)), lambda: start(out(0, 1, 1))],
-        })
-        return carry
-
-    lax.fori_loop(0, COLORS * half, pack, 0)
-    start(out(0, 2, 0) + out(0, 2, 1))
+    start(out(0, *CHUNKS[-1]))
     for k in range(COLORS):
         start(gather(0, k))
     for phase in range(1, 3):
@@ -317,6 +339,7 @@
         at(i, {j: [lambda q=q: arrive(out(2, *q))] for j, q in enumerate(CHUNKS)})
         d[k, sh] = expert_ffn(d[k, sh].reshape(TILE, dim), wg, wu, wd).reshape(SIDE, SIDE, SIDE, PART, dim)
         at(i, {j: [lambda q=q: start(back(2, *q))] for j, q in enumerate(CHUNKS)})
+        at(i, {j + 3: [lambda j=j: arrive(gather(2, j)), lambda j=j: start(gather(4, j))] for j in range(COLORS)})
         return carry
 
     lax.fori_loop(0, len(CHUNKS), ffn, 0)
@@ -327,7 +350,7 @@
 
     def over_ffn(i, carry):
         core, k, part = (s + i // 6) % 2, (i // 2) % COLORS, (i % 2) * 2
-        before = {j: [lambda j=j: arrive(gather(2, j)), lambda j=j: start(gather(3, j))] for j in range(COLORS)}
+        before = {2 * j: [lambda j=j: arrive(gather(4, j)), lambda j=j: start(gather(3, j))] for j in range(COLORS)}
         before.update({6 + 2 * j: [lambda j=j: arrive(gather(3, j))] for j in range(COLORS)})
         at(i, before)
         got = every[core, k, pl.ds(part, 2)].reshape(TILE, dim + TAIL)
@@ -348,9 +371,18 @@
         arrive(reduce(3, k))
         merge(3, k)
         if k:
+            start(reduce(4, k - 1))
+    start(reduce(4, 2))
+    for k, h in CHUNKS[:COLORS]:
+        arrive(back(1, k, h))
+        start(back(0, k, h))
+    for k in range(COLORS):
+        arrive(reduce(4, k))
+        merge(4, k)
+        if k:
             start(reduce(2, k - 1))
     start(reduce(2, 2))
-    for k, h in CHUNKS:
+    for k, h in CHUNKS[COLORS:]:
         arrive(back(1, k, h))
         start(back(0, k, h))
     for phase in (2, 1):
@@ -363,31 +395,32 @@
     total[...] = jnp.zeros_like(total)
 
     def mix(i, carry):
-        at(i, {k: [lambda k=k: arrive(back(0, k, 0)), lambda k=k: arrive(back(0, k, 1))] for k in range(COLORS)})
-        got = aa[i].reshape(rows, dim)
-        lanes = iota((TILE, rows), 1) + i * rows
+        k, sh = i % COLORS, (s + i // COLORS) % 2
+        at(i, {j: [lambda q=q: arrive(back(0, *q))] for j, q in enumerate(CHUNKS)})
+        got = aa[k, sh].reshape(TILE, dim)
+        lanes = (iota((TILE, TILE), 1) + (k * rows + sh * TILE)).astype(jnp.float32)
         for part in range(tok // TILE):
             where = pl.ds(part * TILE, TILE)
-            for slot in range(2):
-                pick = ones_where(pos[where, slot:slot + 1] == lanes)
-                total[where, :] += gate_ref[where, slot:slot + 1] * dot(pick, got)
+            add = cols[where, 2:3] * dot(ones_where(cols[where, 0:1] == lanes), got)
+            total[where, :] += add + cols[where, 3:4] * dot(ones_where(cols[where, 1:2] == lanes), got)
         return carry
 
-    lax.fori_loop(0, COLORS, mix, 0)
+    lax.fori_loop(0, len(CHUNKS), mix, 0)
     last[...] = jnp.zeros_like(last)
     for k in range(COLORS):
         arrive(reduce(0, k))
         merge(0, k)
-    lanes = iota((tok, last.shape[0]), 1) + COLORS * rows
-    more = jnp.zeros((tok, dim), jnp.float32)
-    for slot in range(2):
-        more = more + gate_ref[:, slot:slot + 1] * dot(ones_where(pos[:, slot:slot + 1] == lanes), last[...])
-    y_ref[...] = (total[...] + more).astype(jnp.bfloat16)
+    lanes = (iota((TILE, last.shape[0]), 1) + COLORS * rows).astype(jnp.float32)
+    for part in range(tok // TILE):
+        where = pl.ds(part * TILE, TILE)
+        add = cols[where, 2:3] * dot(ones_where(cols[where, 0:1] == lanes), last[...])
+        add = add + cols[where, 3:4] * dot(ones_where(cols[where, 1:2] == lanes), last[...])
+        y_ref[where, :] = (total[where, :] + add).astype(jnp.bfloat16)
     for k in range(COLORS):
         for phase in range(3):
             for h in range(2):
                 settle(out(phase, k, h) + back(phase, k, h))
-        for phase in range(4):
+        for phase in range(5):
             settle(gather(phase, k) + reduce(phase, k))
 
 
@@ -455,7 +488,7 @@
         sems = pltpu.SemaphoreType.DMA
         main = pltpu.VMEM((COLORS, 2) + cube + (PART, dim), bf16)
         pairs = sems((3, COLORS, 2, SIDE))
-        quads = sems((4, COLORS, SIDE))
+        quads = sems((5, COLORS, SIDE))
         y, flag = pl.pallas_call(
             layer_kernel,
             out_shape=[shape(tok, dim), jax.ShapeDtypeStruct((1, 1), jnp.float32)],
@@ -464,24 +497,24 @@
             scratch_shapes=[
                 pltpu.VMEM((dim, ff), bf16), pltpu.VMEM((dim, ff), bf16), pltpu.VMEM((ff, dim), bf16),
                 main, main, main, main, main, main, main,
-                pltpu.VMEM((COLORS, SPARE, dim + TAIL), bf16),
                 pltpu.VMEM((2, COLORS) + cube + (SPARE, dim + TAIL), bf16),
                 pltpu.VMEM((2, COLORS) + cube + (SPARE, dim), bf16),
                 pltpu.VMEM((COLORS,) + cube + (SPARE, dim), bf16),
                 pltpu.VMEM((COLORS, SIDE, SIDE, SPARE, dim), bf16),
                 pltpu.VMEM((COLORS, SIDE, SPARE, dim), bf16),
-                pltpu.VMEM((COLORS, SIDE - 1, SIDE, SIDE, SPARE, dim), bf16),
+                pltpu.VMEM((COLORS, 2, SIDE // 2, SIDE, SPARE, dim), bf16),
+                pltpu.VMEM((COLORS, 2, SIDE, SIDE, SPARE, dim), bf16),
                 pltpu.VMEM((COLORS, SIDE - 1, SIDE, SPARE, dim), bf16),
                 pltpu.VMEM((COLORS, SIDE - 1, SPARE, dim), bf16),
                 pltpu.VMEM((128, dim), bf16),
-                pltpu.VMEM((tok, 128), jnp.int32),
+                pltpu.VMEM((tok, 128), jnp.float32),
                 pltpu.VMEM((tok, dim), jnp.float32),
-                pairs, pairs, pairs, pairs, quads, quads, quads, quads, sems((3,)), sems((3,)),
+                pairs, pairs, pairs, pairs, quads, quads, quads, quads, sems((3,)),
             ],
             compiler_params=pltpu.CompilerParams(
                 collective_id=0, has_side_effects=True, vmem_limit_bytes=67043328),
             name="layer",
-        )(route, gate, x, w_gate, w_up, w_down)
+        )(route.T, gate.T, x, w_gate, w_up, w_down)
         return lax.cond(flag[0, 0] > 0.0, wide, lambda *args: y, x, route, gate, w_gate, w_up, w_down)
 
     return jax.shard_map(

time: 132 us -> 131 us (level)
  local copies, waits for them, and re-layouts: 5.34 us -> 2.26 us
    unnamed x3 -> x1, local copies, waits for them, and re-layouts: 5.34 us -> 2.26 us
    pallas_call x1, Pallas kernels: 126 us -> 127 us  [device_step(): pl.pallas_call(layer_kernel, out_shape=[shape(tok, dim), jax.ShapeDtypeSt...]
where the time goes in v4:
time: 131 us; the launch traced here: 130 us
  Pallas kernels  127 us (97%)
  local copies, waits for them, and re-layouts  2.26 us (2%)
    pallas_call x1, Pallas kernels, device_step(): pl.pallas_call(layer_kernel, out_shape=[shape(tok, dim), jax.ShapeDtypeSt...  127 us

profile of v4, /device:TPU:1, one launch (start us, length us, event | category | flops | bytes accessed | tf_op | source)
XLA Modules:
  0.0 130.4 jit_solution(8455613983807521497)
XLA Ops:
  0.0 127.3 %layer.1 = (bf16[512,1024]{1,0:T(8,128)(2,1)}, f32[1,1]{1,0:T(1,128)}) custom-call(s32[2,512]{1,0:T(2,128)} %bitcast.19, f32[2,512]{1,0:T(2,128)} %bitcast.20, bf16[512,1024]{1,0:T(8,128)(2,1)} %x_ref.1, bf16[1024,512]{1,0:T(8,128)(2,1)} %bitcast.13, bf16[1024,512]{1,0:T(8,128)(2,1)} %bitcast.15, bf16[512,1024]{1,0:T(8,128)(2,1)} %bitcast.17), custom_call_target="tpu_custom_call" | custom-call | tf_op jit(solution)/shard_map/layer/pallas_call | solution.py:492
  127.9 0.2 conditional.1
  128.1 2.3 %copy.14 = bf16[512,1024]{1,0:T(8,128)(2,1)} copy(bf16[512,1024]{1,0:T(8,128)(2,1)} %get-tuple-element.33) | data formatting | bytes 2097152

commit v5 on v4

--- a/solution.py
+++ b/solution.py
@@ -126,15 +126,8 @@
         copy.start()
 
 
-def arrive(copies):
-    for copy in copies:
-        copy.wait_recv()
-
-
-def settle(copies):
-    for copy in copies:
-        if copy.is_remote:
-            copy.wait_send()
+def drain(ref, sem):
+    pltpu.make_async_copy(ref, ref, sem).wait()
 
 
 def at(i, table):
@@ -156,9 +149,9 @@
     rows = 2 * SIDE ** 3 * PART
     t = Torus()
     s = t.sub
-    load = [pltpu.make_async_copy(src, dst, wsem.at[i])
-            for i, (src, dst) in enumerate(((wg_hbm, wg), (wu_hbm, wu), (wd_hbm, wd)))]
-    start(load)
+    weights = [(src, dst, wsem.at[i]) for i, (src, dst) in enumerate(((wg_hbm, wg), (wu_hbm, wu), (wd_hbm, wd)))]
+    for src, dst, sem in weights:
+        pltpu.make_async_copy(src, dst, sem).start()
     everyone_here = t.greet()
 
     def place(k):
@@ -178,10 +171,9 @@
             else:
                 src, dst = c.at[k, sh, :, :, to], d.at[k, sh, c3]
             if step == 0 and core == 0:
-                copies.append(pltpu.make_async_copy(src, dst, recv.at[phase, k, h, step]))
+                copies.append(pltpu.make_async_copy(src, dst, recv.at[phase, k, h]))
             else:
-                copies.append(remote(src, dst, send.at[phase, k, h, step], recv.at[phase, k, h, step],
-                                     t.device(ax, step, core)))
+                copies.append(remote(src, dst, send.at[phase, h], recv.at[phase, k, h], t.device(ax, step, core)))
         return copies
 
     def back(phase, k, h):
@@ -198,43 +190,45 @@
             else:
                 src, dst = d.at[k, sh, to], cc.at[k, sh, :, :, c3]
             if step == 0 and core == 0:
-                copies.append(pltpu.make_async_copy(src, dst, brecv.at[phase, k, h, step]))
+                copies.append(pltpu.make_async_copy(src, dst, brecv.at[phase, k, h]))
             else:
-                copies.append(remote(src, dst, bsend.at[phase, k, h, step], brecv.at[phase, k, h, step],
-                                     t.device(ax, step, core)))
+                copies.append(remote(src, dst, bsend.at[phase, h], brecv.at[phase, k, h], t.device(ax, step, core)))
         return copies
 
     def gather(phase, k):
         c1, c2, c3 = place(k)
         if phase == 3:
             part = every.at[s, k]
-            return [remote(part, part, esend.at[3, k, 0], erecv.at[3, k, 0], t.device(0, 0, 1))]
+            return [remote(part, part, esend.at[3], erecv.at[3, k], t.device(0, 0, 1))]
         if phase == 4:
             copies = []
             for step, part in ((1, slice(0, SIDE // 2)), (3, slice(SIDE // 2, SIDE))):
                 far = every.at[s, k, part, :, t.coord((k + 2) % 3, -step)]
-                copies.append(remote(far, far, esend.at[4, k, step], erecv.at[4, k, step], t.device((k + 2) % 3, step)))
+                copies.append(remote(far, far, esend.at[4], erecv.at[4, k], t.device((k + 2) % 3, step)))
             return copies
         mine = (every.at[s, k, c1, c2, c3], every.at[s, k, :, c2, c3], every.at[s, k, :, :, c3])[phase]
-        return [remote(mine, mine, esend.at[phase, k, step], erecv.at[phase, k, step],
-                       t.device((k + phase) % 3, step)) for step in (STEPS[:2] if phase == 2 else STEPS)]
+        return [remote(mine, mine, esend.at[phase], erecv.at[phase, k], t.device((k + phase) % 3, step))
+                for step in (STEPS[:2] if phase == 2 else STEPS)]
+
+    def gathered(k):
+        return (every.at[0, k, 0:3, 0, 0], every.at[0, k, 0:3, :, 0], every.at[0, k, 0:2], every.at[0, k],
+                every.at[0, k, 0:1])
 
     def reduce(phase, k):
         if phase == 3:
-            return [remote(late.at[1 - s, k], stage.at[k], rsend.at[3, k, 0], rrecv.at[3, k, 0], t.device(0, 0, 1))]
+            return [remote(late.at[1 - s, k], stage.at[k], rsend.at[3], rrecv.at[3, k], t.device(0, 0, 1))]
         copies = []
         if phase == 4:
             far = t.coord((k + 2) % 3, 2)
             for i, (step, part) in enumerate(((1, slice(0, SIDE // 2)), (3, slice(SIDE // 2, SIDE)))):
-                copies.append(remote(late.at[s, k, part, :, far], relay.at[k, i], rsend.at[4, k, step],
-                                     rrecv.at[4, k, step], t.device((k + 2) % 3, step)))
+                copies.append(remote(late.at[s, k, part, :, far], relay.at[k, i], rsend.at[4],
+                                     rrecv.at[4, k], t.device((k + 2) % 3, step)))
             return copies
         for step in STEPS[:2] if phase == 2 else STEPS:
             to = t.coord((k + phase) % 3, step)
             src = (sum1.at[k, to], sum2.at[k, :, to], late.at[s, k, :, :, to])[phase]
             dst = (got1, got2, got3)[phase].at[k, step // 2 if phase == 2 else step - 1]
-            copies.append(remote(src, dst, rsend.at[phase, k, step], rrecv.at[phase, k, step],
-                                 t.device((k + phase) % 3, step)))
+            copies.append(remote(src, dst, rsend.at[phase], rrecv.at[phase, k], t.device((k + phase) % 3, step)))
         return copies
 
     def merge(phase, k):
@@ -295,19 +289,6 @@
     both = jnp.transpose(jnp.where(iota((tok, 128), 1) == 0, pos0, pos1))
     row0, row1 = both[0:1, :], both[1:2, :]
 
-    def pack(i, carry):
-        k, sh = i % COLORS, (s + i // COLORS) % 2
-        spot = (iota((TILE, tok), 0) + (k * rows + sh * TILE)).astype(jnp.float32)
-        pick = ones_where((spot == row0) | (spot == row1))
-        got = dot(pick, x_ref[...]).astype(jnp.bfloat16)
-        a[k, sh] = got.reshape(SIDE, SIDE, SIDE, PART, dim)
-        events = {j + 1: [lambda q=q: start(out(0, *q))] for j, q in enumerate(CHUNKS[:-1])}
-        events[1].insert(0, everyone_here)
-        at(i, events)
-        return carry
-
-    lax.fori_loop(0, len(CHUNKS), pack, 0)
-
     spot = (iota((32, tok), 0) + COLORS * rows).astype(jnp.float32)
     pick0, pick1 = ones_where(spot == row0), ones_where(spot == row1)
     got = dot(pick0 + pick1, x_ref[...]).astype(jnp.bfloat16)
@@ -321,82 +302,121 @@
         part = slice(k * SPARE, (k + 1) * SPARE)
         every[s, k, c1, c2, c3, :, 0:dim] = got[part, :]
         every[s, k, c1, c2, c3, :, dim:dim + TAIL] = tail[part, :]
-    start(out(0, *CHUNKS[-1]))
-    for k in range(COLORS):
-        start(gather(0, k))
-    for phase in range(1, 3):
-        for k, h in CHUNKS:
-            arrive(out(phase - 1, k, h))
-            start(out(phase, k, h))
-        for k in range(COLORS):
-            arrive(gather(phase - 1, k))
-            start(gather(phase, k))
-    arrive(load)
-
-    def ffn(i, carry):
-        k, h = i % COLORS, i // COLORS
-        sh = (s + h) % 2
-        at(i, {j: [lambda q=q: arrive(out(2, *q))] for j, q in enumerate(CHUNKS)})
-        d[k, sh] = expert_ffn(d[k, sh].reshape(TILE, dim), wg, wu, wd).reshape(SIDE, SIDE, SIDE, PART, dim)
-        at(i, {j: [lambda q=q: start(back(2, *q))] for j, q in enumerate(CHUNKS)})
-        at(i, {j + 3: [lambda j=j: arrive(gather(2, j)), lambda j=j: start(gather(4, j))] for j in range(COLORS)})
+    def relay_gather(phase, k):
+        drain(gathered(k)[phase], erecv.at[phase, k])
+        start(gather({0: 1, 1: 2, 2: 4, 4: 3}[phase], k))
+
+    def relay_out(phase, k, h):
+        drain(d.at[k, 0], recv.at[phase, k, h])
+        start(out(phase + 1, k, h))
+
+    def relay_back(phase, k, h):
+        drain(d.at[k, 0], brecv.at[phase, k, h])
+        start(back(phase - 1, k, h))
+
+    def relay_reduce(phase, k):
+        drain((got1, got2, got3, stage, relay)[phase].at[k], rrecv.at[phase, k])
+        merge(phase, k)
+        if phase:
+            start(reduce({3: 4, 4: 2, 2: 1, 1: 0}[phase], k))
+
+    firsts, seconds = CHUNKS[:COLORS], CHUNKS[COLORS:]
+
+    def pack(i, carry):
+        k, sh = i % COLORS, (s + i // COLORS) % 2
+        spot = (iota((TILE, tok), 0) + (k * rows + sh * TILE)).astype(jnp.float32)
+        pick = ones_where((spot == row0) | (spot == row1))
+        got = dot(pick, x_ref[...]).astype(jnp.bfloat16)
+        a[k, sh] = got.reshape(SIDE, SIDE, SIDE, PART, dim)
+        events = {j + 1: [lambda q=q: start(out(0, *q))] for j, q in enumerate(firsts)}
+        events[1] = [everyone_here] + [lambda k=k: start(gather(0, k)) for k in range(COLORS)] + events[1]
+        at(i, events)
         return carry
 
-    lax.fori_loop(0, len(CHUNKS), ffn, 0)
-
+    lax.fori_loop(0, len(CHUNKS), pack, 0)
+    for k in range(COLORS):
+        relay_gather(0, k)
+    for q in seconds:
+        start(out(0, *q))
+    for k in range(COLORS):
+        relay_gather(1, k)
+    for q in firsts:
+        relay_out(0, *q)
+    for k in range(COLORS):
+        relay_gather(2, k)
+    for q in seconds:
+        relay_out(0, *q)
+    for q in firsts:
+        relay_out(1, *q)
+    for src, dst, sem in weights:
+        pltpu.make_async_copy(src, dst, sem).wait()
     me = (s * SIDE ** 3 + lax.axis_index("ep") + 1).astype(jnp.float32)
     flag_ref[...] = jnp.zeros_like(flag_ref)
-    order = [2, 4, 5, 7, 9, 10]
-
-    def over_ffn(i, carry):
-        core, k, part = (s + i // 6) % 2, (i // 2) % COLORS, (i % 2) * 2
-        before = {2 * j: [lambda j=j: arrive(gather(4, j)), lambda j=j: start(gather(3, j))] for j in range(COLORS)}
-        before.update({6 + 2 * j: [lambda j=j: arrive(gather(3, j))] for j in range(COLORS)})
+
+    over_steps, main_steps = (0, 1, 2, 3, 4, 8), (5, 6, 7, 9, 10, 11)
+    before = {j: [lambda q=q: drain(d.at[q[0], 0], recv.at[2, q[0], q[1]])] for j, q in zip(main_steps, CHUNKS)}
+    before.update({over_steps[COLORS + k]: [lambda k=k: drain(gathered(k)[3], erecv.at[3, k])] for k in range(COLORS)})
+    before[0] = [lambda k=k: relay_gather(4, k) for k in range(COLORS)]
+    before[4].insert(0, lambda: start(reduce(3, 0)))
+    before[5].insert(0, lambda: start(reduce(3, 1)))
+    before[9].insert(0, lambda: start(reduce(3, 2)))
+    after = {j: [lambda q=q: start(back(2, *q))] for j, q in zip(main_steps, CHUNKS)}
+    after[2] = [lambda q=q: relay_out(1, *q) for q in seconds]
+    after[6].append(lambda: relay_reduce(3, 0))
+    after[9].append(lambda: relay_reduce(3, 1))
+    after[11].append(lambda: relay_reduce(3, 2))
+
+    def work(i, carry):
         at(i, before)
-        got = every[core, k, pl.ds(part, 2)].reshape(TILE, dim + TAIL)
-        tail = got[:, dim:dim + TAIL].astype(jnp.float32)
-        flag_ref[...] = jnp.maximum(flag_ref[...], jnp.max(tail[:, 1:2], axis=0, keepdims=True))
-        result = expert_ffn(got[:, 0:dim], wg, wu, wd).astype(jnp.float32)
-        result = jnp.where(tail[:, 0:1] == me, result, 0.0).astype(jnp.bfloat16)
-        late[core, k, pl.ds(part, 2)] = result.reshape(2, SIDE, SIDE, SPARE, dim)
-        at(i, {order[j]: [lambda q=q: arrive(back(2, *q)), lambda q=q: start(back(1, *q))]
-               for j, q in enumerate(CHUNKS)})
-        at(i, {8: [lambda: start(reduce(3, 0))]})
+        is_over = (i < 5) | (i == 8)
+
+        @pl.when(is_over)
+        def _():
+            j = jnp.where(i == 8, 5, i)
+            core, k = (s + j // COLORS) % 2, j % COLORS
+            got = every[core, k].reshape(2 * TILE, dim + TAIL)
+            tail = got[:, dim:dim + TAIL].astype(jnp.float32)
+            flag_ref[...] = jnp.maximum(flag_ref[...], jnp.max(tail[:, 1:2], axis=0, keepdims=True))
+            result = expert_ffn(got[:, 0:dim], wg, wu, wd).astype(jnp.float32)
+            result = jnp.where(tail[:, 0:1] == me, result, 0.0).astype(jnp.bfloat16)
+            late[core, k] = result.reshape(SIDE, SIDE, SIDE, SPARE, dim)
+
+        @pl.when(jnp.logical_not(is_over))
+        def _():
+            j = jnp.where(i < 8, i - 5, i - 6)
+            k, sh = j % COLORS, (s + j // COLORS) % 2
+            d[k, sh] = expert_ffn(d[k, sh].reshape(TILE, dim), wg, wu, wd).reshape(SIDE, SIDE, SIDE, PART, dim)
+
+        at(i, after)
         return carry
 
-    lax.fori_loop(0, 12, over_ffn, 0)
-    start(reduce(3, 1))
-    start(reduce(3, 2))
-    for k in range(COLORS):
-        arrive(reduce(3, k))
-        merge(3, k)
-        if k:
-            start(reduce(4, k - 1))
-    start(reduce(4, 2))
-    for k, h in CHUNKS[:COLORS]:
-        arrive(back(1, k, h))
-        start(back(0, k, h))
-    for k in range(COLORS):
-        arrive(reduce(4, k))
-        merge(4, k)
-        if k:
-            start(reduce(2, k - 1))
-    start(reduce(2, 2))
-    for k, h in CHUNKS[COLORS:]:
-        arrive(back(1, k, h))
-        start(back(0, k, h))
-    for phase in (2, 1):
-        for k in range(COLORS):
-            arrive(reduce(phase, k))
-            merge(phase, k)
-            if k:
-                start(reduce(phase - 1, k - 1))
-        start(reduce(phase - 1, 2))
-    total[...] = jnp.zeros_like(total)
+    lax.fori_loop(0, 12, work, 0)
+    for q in firsts:
+        relay_back(2, *q)
+    for k in range(COLORS):
+        relay_reduce(4, k)
+    for q in seconds:
+        relay_back(2, *q)
+    for k in range(COLORS):
+        relay_reduce(2, k)
+    for q in firsts:
+        relay_back(1, *q)
+    for k in range(COLORS):
+        relay_reduce(1, k)
+    for q in seconds:
+        relay_back(1, *q)
+    last[...] = jnp.zeros_like(last)
+    for k in range(COLORS):
+        relay_reduce(0, k)
+    lanes = (iota((TILE, last.shape[0]), 1) + COLORS * rows).astype(jnp.float32)
+    for part in range(tok // TILE):
+        where = pl.ds(part * TILE, TILE)
+        add = cols[where, 2:3] * dot(ones_where(cols[where, 0:1] == lanes), last[...])
+        total[where, :] = add + cols[where, 3:4] * dot(ones_where(cols[where, 1:2] == lanes), last[...])
 
     def mix(i, carry):
         k, sh = i % COLORS, (s + i // COLORS) % 2
-        at(i, {j: [lambda q=q: arrive(back(0, *q))] for j, q in enumerate(CHUNKS)})
+        at(i, {j: [lambda q=q: drain(d.at[q[0], 0], brecv.at[0, q[0], q[1]])] for j, q in enumerate(CHUNKS)})
         got = aa[k, sh].reshape(TILE, dim)
         lanes = (iota((TILE, TILE), 1) + (k * rows + sh * TILE)).astype(jnp.float32)
         for part in range(tok // TILE):
@@ -406,22 +426,15 @@
         return carry
 
     lax.fori_loop(0, len(CHUNKS), mix, 0)
-    last[...] = jnp.zeros_like(last)
-    for k in range(COLORS):
-        arrive(reduce(0, k))
-        merge(0, k)
-    lanes = (iota((TILE, last.shape[0]), 1) + COLORS * rows).astype(jnp.float32)
-    for part in range(tok // TILE):
-        where = pl.ds(part * TILE, TILE)
-        add = cols[where, 2:3] * dot(ones_where(cols[where, 0:1] == lanes), last[...])
-        add = add + cols[where, 3:4] * dot(ones_where(cols[where, 1:2] == lanes), last[...])
-        y_ref[where, :] = (total[where, :] + add).astype(jnp.bfloat16)
-    for k in range(COLORS):
-        for phase in range(3):
-            for h in range(2):
-                settle(out(phase, k, h) + back(phase, k, h))
-        for phase in range(5):
-            settle(gather(phase, k) + reduce(phase, k))
+    y_ref[...] = total[...].astype(jnp.bfloat16)
+    for phase in range(3):
+        for h in range(2):
+            sent = d.at[:, 0] if phase == 0 and h else d.at[:, 0, 0:3]
+            drain(sent, send.at[phase, h])
+            drain(sent, bsend.at[phase, h])
+    for phase in range(5):
+        drain(gathered(slice(None))[phase], esend.at[phase])
+        drain((got1, got2, got3, stage, relay)[phase], rsend.at[phase])
 
 
 def solution(mesh):
@@ -487,8 +500,8 @@
         w_gate, w_up, w_down = w_gate[0], w_up[0], w_down[0]
         sems = pltpu.SemaphoreType.DMA
         main = pltpu.VMEM((COLORS, 2) + cube + (PART, dim), bf16)
-        pairs = sems((3, COLORS, 2, SIDE))
-        quads = sems((5, COLORS, SIDE))
+        one_way = sems((3, COLORS, 2))
+        late_in, late_out = sems((5, COLORS)), sems((5,))
         y, flag = pl.pallas_call(
             layer_kernel,
             out_shape=[shape(tok, dim), jax.ShapeDtypeStruct((1, 1), jnp.float32)],
@@ -509,7 +522,7 @@
                 pltpu.VMEM((128, dim), bf16),
                 pltpu.VMEM((tok, 128), jnp.float32),
                 pltpu.VMEM((tok, dim), jnp.float32),
-                pairs, pairs, pairs, pairs, quads, quads, quads, quads, sems((3,)),
+                sems((3, 2)), one_way, sems((3, 2)), one_way, late_out, late_in, late_out, late_in, sems((3,)),
             ],
             compiler_params=pltpu.CompilerParams(
                 collective_id=0, has_side_effects=True, vmem_limit_bytes=67043328),

time: 131 us -> 112 us (0.85)
  Pallas kernels: 127 us -> 108 us
    pallas_call x1, Pallas kernels: 127 us -> 108 us  [device_step(): pl.pallas_call(layer_kernel, out_shape=[shape(tok, dim), jax.ShapeDtypeSt...]
where the time goes in v5:
time: 112 us
  Pallas kernels  108 us (96%)
  local copies, waits for them, and re-layouts  2.26 us (2%)
    pallas_call x1, Pallas kernels, device_step(): pl.pallas_call(layer_kernel, out_shape=[shape(tok, dim), jax.ShapeDtypeSt...  108 us
    unnamed x1, local copies, waits for them, and re-layouts  2.26 us

profile of v5, /device:TPU:1, one launch (start us, length us, event | category | flops | bytes accessed | tf_op | source)
XLA Modules:
  0.0 111.6 jit_solution(7871543121141452569)
XLA Ops:
  0.0 108.5 %layer.1 = (bf16[512,1024]{1,0:T(8,128)(2,1)}, f32[1,1]{1,0:T(1,128)}) custom-call(s32[2,512]{1,0:T(2,128)} %bitcast.19, f32[2,512]{1,0:T(2,128)} %bitcast.20, bf16[512,1024]{1,0:T(8,128)(2,1)} %x_ref.1, bf16[1024,512]{1,0:T(8,128)(2,1)} %bitcast.13, bf16[1024,512]{1,0:T(8,128)(2,1)} %bitcast.15, bf16[512,1024]{1,0:T(8,128)(2,1)} %bitcast.17), custom_call_target="tpu_custom_call" | custom-call | tf_op jit(solution)/shard_map/layer/pallas_call | solution.py:505
  109.1 0.2 conditional.1
  109.4 2.3 %copy.14 = bf16[512,1024]{1,0:T(8,128)(2,1)} copy(bf16[512,1024]{1,0:T(8,128)(2,1)} %get-tuple-element.33) | data formatting | bytes 2097152

commit v6 on v5

--- a/solution.py
+++ b/solution.py
@@ -10,6 +10,7 @@
 MESH = pl.DeviceIdType.MESH
 TILE = 256
 VMEM_LIMIT = 60 * 1024 * 1024
+LAYER_VMEM = 58 * 1024 * 1024
 COLORS = 3
 PART = 4
 BASE = COLORS * PART
@@ -142,17 +143,18 @@
 CHUNKS = [(k, h) for h in range(2) for k in range(COLORS)]
 
 
-def layer_kernel(route_ref, gate_ref, x_ref, wg_hbm, wu_hbm, wd_hbm, y_ref, flag_ref,
-                 wg, wu, wd, a, b, c, d, cc, bb, aa, every, late, stage, sum2, sum1, relay, got3, got2, got1, last,
+def layer_kernel(route_ref, gate_ref, x_hbm, wg_hbm, wu_hbm, wd_hbm, y_ref, flag_ref,
+                 x_ref, wg, wu, wd, a, b, c, d, cc, bb, aa, every, late, stage, sum2, sum1, relay, got3, got2, got1, last,
                  cols, total, send, recv, bsend, brecv, esend, erecv, rsend, rrecv, wsem):
     tok, dim = x_ref.shape
     rows = 2 * SIDE ** 3 * PART
     t = Torus()
     s = t.sub
-    weights = [(src, dst, wsem.at[i]) for i, (src, dst) in enumerate(((wg_hbm, wg), (wu_hbm, wu), (wd_hbm, wd)))]
-    for src, dst, sem in weights:
+    everyone_here = t.greet()
+    inputs = ((x_hbm, x_ref), (wg_hbm, wg), (wu_hbm, wu), (wd_hbm, wd))
+    x_load, *weights = [(src, dst, wsem.at[i]) for i, (src, dst) in enumerate(inputs)]
+    for src, dst, sem in (x_load, *weights):
         pltpu.make_async_copy(src, dst, sem).start()
-    everyone_here = t.greet()
 
     def place(k):
         return tuple(t.at[(k + i) % 3] for i in range(3))
@@ -289,19 +291,6 @@
     both = jnp.transpose(jnp.where(iota((tok, 128), 1) == 0, pos0, pos1))
     row0, row1 = both[0:1, :], both[1:2, :]
 
-    spot = (iota((32, tok), 0) + COLORS * rows).astype(jnp.float32)
-    pick0, pick1 = ones_where(spot == row0), ones_where(spot == row1)
-    got = dot(pick0 + pick1, x_ref[...]).astype(jnp.bfloat16)
-    expert0 = jnp.broadcast_to(route0 + 1, (tok, TAIL)).astype(jnp.bfloat16)
-    expert1 = jnp.broadcast_to(route1 + 1, (tok, TAIL)).astype(jnp.bfloat16)
-    owner = dot(pick0, expert0) + dot(pick1, expert1)
-    flag = jnp.where(n_over > OVER, 1.0, 0.0)
-    tail = jnp.where(iota((32, TAIL), 1) == 0, owner, flag).astype(jnp.bfloat16)
-    for k in range(COLORS):
-        c1, c2, c3 = place(k)
-        part = slice(k * SPARE, (k + 1) * SPARE)
-        every[s, k, c1, c2, c3, :, 0:dim] = got[part, :]
-        every[s, k, c1, c2, c3, :, dim:dim + TAIL] = tail[part, :]
     def relay_gather(phase, k):
         drain(gathered(k)[phase], erecv.at[phase, k])
         start(gather({0: 1, 1: 2, 2: 4, 4: 3}[phase], k))
@@ -321,6 +310,21 @@
             start(reduce({3: 4, 4: 2, 2: 1, 1: 0}[phase], k))
 
     firsts, seconds = CHUNKS[:COLORS], CHUNKS[COLORS:]
+
+    def pack_over():
+        spot = (iota((32, tok), 0) + COLORS * rows).astype(jnp.float32)
+        pick0, pick1 = ones_where(spot == row0), ones_where(spot == row1)
+        got = dot(pick0 + pick1, x_ref[...]).astype(jnp.bfloat16)
+        expert0 = jnp.broadcast_to(route0 + 1, (tok, TAIL)).astype(jnp.bfloat16)
+        expert1 = jnp.broadcast_to(route1 + 1, (tok, TAIL)).astype(jnp.bfloat16)
+        owner = dot(pick0, expert0) + dot(pick1, expert1)
+        flag = jnp.where(n_over > OVER, 1.0, 0.0)
+        tail = jnp.where(iota((32, TAIL), 1) == 0, owner, flag).astype(jnp.bfloat16)
+        for k in range(COLORS):
+            c1, c2, c3 = place(k)
+            part = slice(k * SPARE, (k + 1) * SPARE)
+            every[s, k, c1, c2, c3, :, 0:dim] = got[part, :]
+            every[s, k, c1, c2, c3, :, dim:dim + TAIL] = tail[part, :]
 
     def pack(i, carry):
         k, sh = i % COLORS, (s + i // COLORS) % 2
@@ -333,6 +337,8 @@
         at(i, events)
         return carry
 
+    pltpu.make_async_copy(*x_load).wait()
+    pack_over()
     lax.fori_loop(0, len(CHUNKS), pack, 0)
     for k in range(COLORS):
         relay_gather(0, k)
@@ -414,19 +420,27 @@
         add = cols[where, 2:3] * dot(ones_where(cols[where, 0:1] == lanes), last[...])
         total[where, :] = add + cols[where, 3:4] * dot(ones_where(cols[where, 1:2] == lanes), last[...])
 
-    def mix(i, carry):
+    def mix(i, final=False):
         k, sh = i % COLORS, (s + i // COLORS) % 2
-        at(i, {j: [lambda q=q: drain(d.at[q[0], 0], brecv.at[0, q[0], q[1]])] for j, q in enumerate(CHUNKS)})
         got = aa[k, sh].reshape(TILE, dim)
         lanes = (iota((TILE, TILE), 1) + (k * rows + sh * TILE)).astype(jnp.float32)
         for part in range(tok // TILE):
             where = pl.ds(part * TILE, TILE)
             add = cols[where, 2:3] * dot(ones_where(cols[where, 0:1] == lanes), got)
-            total[where, :] += add + cols[where, 3:4] * dot(ones_where(cols[where, 1:2] == lanes), got)
+            add = add + cols[where, 3:4] * dot(ones_where(cols[where, 1:2] == lanes), got)
+            if final:
+                y_ref[where, :] = (total[where, :] + add).astype(jnp.bfloat16)
+            else:
+                total[where, :] += add
+
+    def mix_early(i, carry):
+        at(i, {j: [lambda q=q: drain(d.at[q[0], 0], brecv.at[0, q[0], q[1]])] for j, q in enumerate(CHUNKS)})
+        mix(i)
         return carry
 
-    lax.fori_loop(0, len(CHUNKS), mix, 0)
-    y_ref[...] = total[...].astype(jnp.bfloat16)
+    lax.fori_loop(0, len(CHUNKS) - 1, mix_early, 0)
+    drain(d.at[0, 0], brecv.at[0, CHUNKS[-1][0], CHUNKS[-1][1]])
+    mix(len(CHUNKS) - 1, final=True)
     for phase in range(3):
         for h in range(2):
             sent = d.at[:, 0] if phase == 0 and h else d.at[:, 0, 0:3]
@@ -504,10 +518,11 @@
         late_in, late_out = sems((5, COLORS)), sems((5,))
         y, flag = pl.pallas_call(
             layer_kernel,
-            out_shape=[shape(tok, dim), jax.ShapeDtypeStruct((1, 1), jnp.float32)],
-            in_specs=[vmem, vmem, vmem, hbm, hbm, hbm],
+            out_shape=[pltpu.VMEM((tok, dim), bf16), jax.ShapeDtypeStruct((1, 1), jnp.float32)],
+            in_specs=[vmem, vmem, hbm, hbm, hbm, hbm],
             out_specs=[vmem, vmem],
             scratch_shapes=[
+                pltpu.VMEM((tok, dim), bf16),
                 pltpu.VMEM((dim, ff), bf16), pltpu.VMEM((dim, ff), bf16), pltpu.VMEM((ff, dim), bf16),
                 main, main, main, main, main, main, main,
                 pltpu.VMEM((2, COLORS) + cube + (SPARE, dim + TAIL), bf16),
@@ -522,10 +537,10 @@
                 pltpu.VMEM((128, dim), bf16),
                 pltpu.VMEM((tok, 128), jnp.float32),
                 pltpu.VMEM((tok, dim), jnp.float32),
-                sems((3, 2)), one_way, sems((3, 2)), one_way, late_out, late_in, late_out, late_in, sems((3,)),
+                sems((3, 2)), one_way, sems((3, 2)), one_way, late_out, late_in, late_out, late_in, sems((4,)),
             ],
             compiler_params=pltpu.CompilerParams(
-                collective_id=0, has_side_effects=True, vmem_limit_bytes=67043328),
+                collective_id=0, has_side_effects=True, vmem_limit_bytes=LAYER_VMEM),
             name="layer",
         )(route.T, gate.T, x, w_gate, w_up, w_down)
         return lax.cond(flag[0, 0] > 0.0, wide, lambda *args: y, x, route, gate, w_gate, w_up, w_down)

time: 112 us -> 109 us (0.973)
  local copies, waits for them, and re-layouts: 2.26 us -> 0.97 us
    unnamed x1, local copies, waits for them, and re-layouts: 2.26 us -> 0.97 us
where the time goes in v6:
time: 109 us
  Pallas kernels  107 us (98%)
    pallas_call x1, Pallas kernels, device_step(): pl.pallas_call(layer_kernel, out_shape=[pltpu.VMEM((tok, dim), bf16), jax...  107 us

profile of v6, /device:TPU:1, one launch (start us, length us, event | category | flops | bytes accessed | tf_op | source)
XLA Modules:
  0.0 109.2 jit_solution(5786852910288504432)
XLA Ops:
  0.0 107.4 %layer.1 = (bf16[512,1024]{1,0:T(8,128)(2,1)S(1)}, f32[1,1]{1,0:T(1,128)}) custom-call(s32[2,512]{1,0:T(2,128)} %bitcast.19, f32[2,512]{1,0:T(2,128)} %bitcast.20, bf16[512,1024]{1,0:T(8,128)(2,1)} %x_hbm.1, bf16[1024,512]{1,0:T(8,128)(2,1)} %bitcast.13, bf16[1024,512]{1,0:T(8,128)(2,1)} %bitcast.15, bf16[512,1024]{1,0:T(8,128)(2,1)} %bitcast.17), custom_call_target="tpu_custom_call" | custom-call | tf_op jit(solution)/shard_map/layer/pallas_call | solution.py:519
  108.0 0.2 conditional.1
  108.3 1.0 copy.14

commit v7 on v6

--- a/solution.py
+++ b/solution.py
@@ -122,6 +122,14 @@
         src_ref=src, dst_ref=dst, send_sem=send_sem, recv_sem=recv_sem, device_id=device, device_id_type=MESH)
 
 
+class Stay:
+    def __init__(self, src, dst):
+        self.src, self.dst = src, dst
+
+    def start(self):
+        self.dst[...] = self.src[...]
+
+
 def start(copies):
     for copy in copies:
         copy.start()
@@ -144,8 +152,8 @@
 
 
 def layer_kernel(route_ref, gate_ref, x_hbm, wg_hbm, wu_hbm, wd_hbm, y_ref, flag_ref,
-                 x_ref, wg, wu, wd, a, b, c, d, cc, bb, aa, every, late, stage, sum2, sum1, relay, got3, got2, got1, last,
-                 cols, total, send, recv, bsend, brecv, esend, erecv, rsend, rrecv, wsem):
+                 x_ref, wg, wu, wd, a, b, c, d, cc, bb, aa, every, note, late, stage, sum2, sum1, relay, got3, got2, got1, last,
+                 cols, total, send, recv, bsend, brecv, esend, erecv, rsend, rrecv, nsend, nrecv, wsem):
     tok, dim = x_ref.shape
     rows = 2 * SIDE ** 3 * PART
     t = Torus()
@@ -173,7 +181,7 @@
             else:
                 src, dst = c.at[k, sh, :, :, to], d.at[k, sh, c3]
             if step == 0 and core == 0:
-                copies.append(pltpu.make_async_copy(src, dst, recv.at[phase, k, h]))
+                copies.append(Stay(src, dst))
             else:
                 copies.append(remote(src, dst, send.at[phase, h], recv.at[phase, k, h], t.device(ax, step, core)))
         return copies
@@ -192,29 +200,46 @@
             else:
                 src, dst = d.at[k, sh, to], cc.at[k, sh, :, :, c3]
             if step == 0 and core == 0:
-                copies.append(pltpu.make_async_copy(src, dst, brecv.at[phase, k, h]))
+                copies.append(Stay(src, dst))
             else:
                 copies.append(remote(src, dst, bsend.at[phase, h], brecv.at[phase, k, h], t.device(ax, step, core)))
         return copies
 
+    def spread(rows_of, phase, k, send_sem, recv_sem):
+        c1, c2, c3 = place(k)
+        ax = (k + min(phase, 2)) % 3
+        if phase == 3:
+            part = rows_of.at[s, k]
+            return [remote(part, part, send_sem, recv_sem, t.device(0, 0, 1))]
+        if phase == 4:
+            ax, copies = (k + 2) % 3, []
+            for step, part in ((1, slice(0, SIDE // 2)), (3, slice(SIDE // 2, SIDE))):
+                far = rows_of.at[s, k, part, :, t.coord(ax, -step)]
+                copies.append(remote(far, far, send_sem, recv_sem, t.device(ax, step)))
+            return copies
+        mine = (rows_of.at[s, k, c1, c2, c3], rows_of.at[s, k, :, c2, c3], rows_of.at[s, k, :, :, c3])[phase]
+        return [remote(mine, mine, send_sem, recv_sem, t.device(ax, step))
+                for step in (STEPS[:2] if phase == 2 else STEPS)]
+
     def gather(phase, k):
-        c1, c2, c3 = place(k)
-        if phase == 3:
-            part = every.at[s, k]
-            return [remote(part, part, esend.at[3], erecv.at[3, k], t.device(0, 0, 1))]
-        if phase == 4:
-            copies = []
-            for step, part in ((1, slice(0, SIDE // 2)), (3, slice(SIDE // 2, SIDE))):
-                far = every.at[s, k, part, :, t.coord((k + 2) % 3, -step)]
-                copies.append(remote(far, far, esend.at[4], erecv.at[4, k], t.device((k + 2) % 3, step)))
-            return copies
-        mine = (every.at[s, k, c1, c2, c3], every.at[s, k, :, c2, c3], every.at[s, k, :, :, c3])[phase]
-        return [remote(mine, mine, esend.at[phase], erecv.at[phase, k], t.device((k + phase) % 3, step))
-                for step in (STEPS[:2] if phase == 2 else STEPS)]
-
-    def gathered(k):
-        return (every.at[0, k, 0:3, 0, 0], every.at[0, k, 0:3, :, 0], every.at[0, k, 0:2], every.at[0, k],
-                every.at[0, k, 0:1])
+        copies = spread(every, phase, k, esend.at[phase], erecv.at[phase, k])
+        if k == 0:
+            copies = spread(note, phase, 0, nsend.at[phase], nrecv.at[phase]) + copies
+        return copies
+
+    def gathered(rows_of, k):
+        return (rows_of.at[0, k, 0:3, 0, 0], rows_of.at[0, k, 0:3, :, 0], rows_of.at[0, k, 0:2], rows_of.at[0, k],
+                rows_of.at[0, k, 0:1])
+
+    def await_gather(phase, k):
+        drain(gathered(every, k)[phase], erecv.at[phase, k])
+        if k == 0:
+            drain(gathered(note, 0)[phase], nrecv.at[phase])
+
+    def turn_note(core):
+        for i in range(SIDE):
+            note[core, 1, :, :, i] = note[core, 0, i]
+            note[core, 2, i] = note[core, 0, :, :, i]
 
     def reduce(phase, k):
         if phase == 3:
@@ -292,15 +317,18 @@
     row0, row1 = both[0:1, :], both[1:2, :]
 
     def relay_gather(phase, k):
-        drain(gathered(k)[phase], erecv.at[phase, k])
+        await_gather(phase, k)
         start(gather({0: 1, 1: 2, 2: 4, 4: 3}[phase], k))
 
+    def brought(phase, k, h):
+        return d.at[k, 0] if phase == 0 and h else d.at[k, 0, 0:3]
+
     def relay_out(phase, k, h):
-        drain(d.at[k, 0], recv.at[phase, k, h])
+        drain(brought(phase, k, h), recv.at[phase, k, h])
         start(out(phase + 1, k, h))
 
     def relay_back(phase, k, h):
-        drain(d.at[k, 0], brecv.at[phase, k, h])
+        drain(brought(phase, k, h), brecv.at[phase, k, h])
         start(back(phase - 1, k, h))
 
     def relay_reduce(phase, k):
@@ -318,13 +346,14 @@
         expert0 = jnp.broadcast_to(route0 + 1, (tok, TAIL)).astype(jnp.bfloat16)
         expert1 = jnp.broadcast_to(route1 + 1, (tok, TAIL)).astype(jnp.bfloat16)
         owner = dot(pick0, expert0) + dot(pick1, expert1)
-        flag = jnp.where(n_over > OVER, 1.0, 0.0)
-        tail = jnp.where(iota((32, TAIL), 1) == 0, owner, flag).astype(jnp.bfloat16)
+        lane = iota((SPARE, TAIL), 1)
+        mark = jnp.where(lane == COLORS, jnp.where(n_over > OVER, 1.0, 0.0), 0.0)
         for k in range(COLORS):
             c1, c2, c3 = place(k)
             part = slice(k * SPARE, (k + 1) * SPARE)
-            every[s, k, c1, c2, c3, :, 0:dim] = got[part, :]
-            every[s, k, c1, c2, c3, :, dim:dim + TAIL] = tail[part, :]
+            every[s, k, c1, c2, c3] = got[part, :]
+            mark = jnp.where(lane == k, owner[part, :], mark)
+        note[s, 0, t.at[0], t.at[1], t.at[2]] = mark.astype(jnp.bfloat16)
 
     def pack(i, carry):
         k, sh = i % COLORS, (s + i // COLORS) % 2
@@ -360,9 +389,11 @@
     flag_ref[...] = jnp.zeros_like(flag_ref)
 
     over_steps, main_steps = (0, 1, 2, 3, 4, 8), (5, 6, 7, 9, 10, 11)
-    before = {j: [lambda q=q: drain(d.at[q[0], 0], recv.at[2, q[0], q[1]])] for j, q in zip(main_steps, CHUNKS)}
-    before.update({over_steps[COLORS + k]: [lambda k=k: drain(gathered(k)[3], erecv.at[3, k])] for k in range(COLORS)})
+    before = {j: [lambda q=q: drain(brought(2, *q), recv.at[2, q[0], q[1]])] for j, q in zip(main_steps, CHUNKS)}
+    before.update({over_steps[COLORS + k]: [lambda k=k: await_gather(3, k)] for k in range(COLORS)})
     before[0] = [lambda k=k: relay_gather(4, k) for k in range(COLORS)]
+    before[0].append(lambda: turn_note(s))
+    before[over_steps[COLORS]].append(lambda: turn_note(1 - s))
     before[4].insert(0, lambda: start(reduce(3, 0)))
     before[5].insert(0, lambda: start(reduce(3, 1)))
     before[9].insert(0, lambda: start(reduce(3, 2)))
@@ -380,11 +411,12 @@
         def _():
             j = jnp.where(i == 8, 5, i)
             core, k = (s + j // COLORS) % 2, j % COLORS
-            got = every[core, k].reshape(2 * TILE, dim + TAIL)
-            tail = got[:, dim:dim + TAIL].astype(jnp.float32)
-            flag_ref[...] = jnp.maximum(flag_ref[...], jnp.max(tail[:, 1:2], axis=0, keepdims=True))
-            result = expert_ffn(got[:, 0:dim], wg, wu, wd).astype(jnp.float32)
-            result = jnp.where(tail[:, 0:1] == me, result, 0.0).astype(jnp.bfloat16)
+            got = every[core, k].reshape(2 * TILE, dim)
+            tail = note[core, k].reshape(2 * TILE, TAIL).astype(jnp.float32)
+            flag_ref[...] = jnp.maximum(flag_ref[...], jnp.max(tail[:, COLORS:COLORS + 1], axis=0, keepdims=True))
+            owner = jnp.sum(jnp.where(iota(tail.shape, 1) == k, tail, 0.0), axis=1, keepdims=True)
+            result = expert_ffn(got, wg, wu, wd).astype(jnp.float32)
+            result = jnp.where(owner == me, result, 0.0).astype(jnp.bfloat16)
             late[core, k] = result.reshape(SIDE, SIDE, SIDE, SPARE, dim)
 
         @pl.when(jnp.logical_not(is_over))
@@ -434,12 +466,12 @@
                 total[where, :] += add
 
     def mix_early(i, carry):
-        at(i, {j: [lambda q=q: drain(d.at[q[0], 0], brecv.at[0, q[0], q[1]])] for j, q in enumerate(CHUNKS)})
+        at(i, {j: [lambda q=q: drain(brought(0, *q), brecv.at[0, q[0], q[1]])] for j, q in enumerate(CHUNKS)})
         mix(i)
         return carry
 
     lax.fori_loop(0, len(CHUNKS) - 1, mix_early, 0)
-    drain(d.at[0, 0], brecv.at[0, CHUNKS[-1][0], CHUNKS[-1][1]])
+    drain(brought(0, *CHUNKS[-1]), brecv.at[0, CHUNKS[-1][0], CHUNKS[-1][1]])
     mix(len(CHUNKS) - 1, final=True)
     for phase in range(3):
         for h in range(2):
@@ -447,7 +479,8 @@
             drain(sent, send.at[phase, h])
             drain(sent, bsend.at[phase, h])
     for phase in range(5):
-        drain(gathered(slice(None))[phase], esend.at[phase])
+        drain(gathered(every, slice(None))[phase], esend.at[phase])
+        drain(gathered(note, 0)[phase], nsend.at[phase])
         drain((got1, got2, got3, stage, relay)[phase], rsend.at[phase])
 
 
@@ -525,7 +558,8 @@
                 pltpu.VMEM((tok, dim), bf16),
                 pltpu.VMEM((dim, ff), bf16), pltpu.VMEM((dim, ff), bf16), pltpu.VMEM((ff, dim), bf16),
                 main, main, main, main, main, main, main,
-                pltpu.VMEM((2, COLORS) + cube + (SPARE, dim + TAIL), bf16),
+                pltpu.VMEM((2, COLORS) + cube + (SPARE, dim), bf16),
+                pltpu.VMEM((2, COLORS) + cube + (SPARE, TAIL), bf16),
                 pltpu.VMEM((2, COLORS) + cube + (SPARE, dim), bf16),
                 pltpu.VMEM((COLORS,) + cube + (SPARE, dim), bf16),
                 pltpu.VMEM((COLORS, SIDE, SIDE, SPARE, dim), bf16),
@@ -537,7 +571,7 @@
                 pltpu.VMEM((128, dim), bf16),
                 pltpu.VMEM((tok, 128), jnp.float32),
                 pltpu.VMEM((tok, dim), jnp.float32),
-                sems((3, 2)), one_way, sems((3, 2)), one_way, late_out, late_in, late_out, late_in, sems((4,)),
+                sems((3, 2)), one_way, sems((3, 2)), one_way, late_out, late_in, late_out, late_in, late_out, late_out, sems((4,)),
             ],
             compiler_params=pltpu.CompilerParams(
                 collective_id=0, has_side_effects=True, vmem_limit_bytes=LAYER_VMEM),

time: 109 us -> 109 us (level)
  no operation moved by 1% of the time
where the time goes in v7:
time: 109 us
  Pallas kernels  107 us (98%)
    pallas_call x1, Pallas kernels, device_step(): pl.pallas_call(layer_kernel, out_shape=[pltpu.VMEM((tok, dim), bf16), jax...  107 us

profile of v7, /device:TPU:1, one launch (start us, length us, event | category | flops | bytes accessed | tf_op | source)
XLA Modules:
  0.0 108.6 jit_solution(12669469110880872451)
XLA Ops:
  0.0 106.8 %layer.1 = (bf16[512,1024]{1,0:T(8,128)(2,1)S(1)}, f32[1,1]{1,0:T(1,128)}) custom-call(s32[2,512]{1,0:T(2,128)} %bitcast.19, f32[2,512]{1,0:T(2,128)} %bitcast.20, bf16[512,1024]{1,0:T(8,128)(2,1)} %x_hbm.1, bf16[1024,512]{1,0:T(8,128)(2,1)} %bitcast.13, bf16[1024,512]{1,0:T(8,128)(2,1)} %bitcast.15, bf16[512,1024]{1,0:T(8,128)(2,1)} %bitcast.17), custom_call_target="tpu_custom_call" | custom-call | tf_op jit(solution)/shard_map/layer/pallas_call | solution.py:552
  107.4 0.2 conditional.1
  107.7 1.0 copy.14
